TPU v7x, 32 devices: a whole 2x2x4 slice. The times are simulated.
32 devices in a mesh: wide: 8 (over z, y), narrow: 4 (over x, core).
Axes of the slice: x: 2, y: 2, z: 4, core: 2. Of those that a mesh axis runs over, the one named last changes fastest.
Arguments:
- checkpoint_slots: float32 [4, 2, 256, 4096], P('narrow', None, 'wide'), may hold values from 0 to 2
- owner_slot: int32 [2], replicated, may hold values from 0 to 3
- row_velocity: float32 [256, 4096], P('wide', 'narrow'), may hold values from -0.4 to 0.4
- column_velocity: float32 [256, 4096], P('wide', 'narrow'), may hold values from -0.4 to 0.4
- land_sea: int32 [256, 4096], P('wide', 'narrow'), may hold values 0 or 1
- layer_class: int32 [2], replicated, may hold values from 0 to 3
- class_speed: float32 [4], replicated, may hold values from 0.05 to 0.6
- final_adjoint: float32 [2, 256, 4096], P(None, 'wide', 'narrow'), may hold values from -6 to 6
- deposit_weight: float32 [256, 4096], P('wide', 'narrow'), may hold values from -6 to 6
Outputs:
- initial_adjoint: float32 [2, 256, 4096], P(None, 'wide', 'narrow')
All inputs are finite; a program needn't handle non-finite values. No bound on the sum of `land_sea` on one device may be relied on, other than what follows from the above.
Results may differ from a plain program's by a relative error of at most 0.00002.
Values sent between devices are 32-bit elements; how exact they have to be, the bound alone decides.
A program may use at most 64 MiB of HBM per device.

v0:
```python
import functools

import jax
import jax.numpy as jnp
from jax import lax
from jax.experimental import pallas as pl
from jax.experimental.pallas import tpu as pltpu
from jax.sharding import PartitionSpec as P

STEPS = 3
RIM = 2
LANES = 128
ROWS = 8
MESH = pl.DeviceIdType.MESH


def stencil_weights(velocity):
    p = jnp.maximum(velocity, 0.0)
    q = jnp.minimum(velocity, 0.0)
    pp = p * p
    qq = q * q
    return [
        0.5 * pp - 0.5 * p,
        2.0 * p - pp,
        0.5 * pp - 1.5 * p + 0.5 * qq + 1.5 * q,
        -2.0 * q - qq,
        0.5 * qq + 0.5 * q,
    ]


def kernel(
    group_wide,
    group,
    owner_hbm,
    class_hbm,
    speed_hbm,
    slots_ref,
    row_velocity_hbm,
    column_velocity_hbm,
    sea_hbm,
    final_hbm,
    deposit_hbm,
    out_ref,
    owner_ref,
    class_ref,
    speed_ref,
    row_velocity_ref,
    column_velocity_ref,
    sea_ref,
    final_ref,
    deposit_ref,
    mine,
    load_sems,
    mine_sems,
    near,
    mixed,
    far,
    field,
    slope,
    grad,
    wr,
    wc,
    centre,
    sea,
    row_send,
    row_recv,
    col_send,
    col_recv,
    near_sems,
    far_sems,
    halo_send_sems,
    halo_recv_sems,
):
    layers, height, breadth = out_ref.shape
    offsets = (-2, -1, 1, 2)
    pair = 2 if group % 2 == 0 else 1
    chips = group // pair
    w = lax.axis_index("wide")
    n = lax.axis_index("narrow")
    chip = lax.div(n, pair)
    core = lax.rem(n, pair)
    blocks = [(slice(r, r + ROWS), r) for r in range(0, height, ROWS)]

    has = {
        ("row", 0): w > 0,
        ("row", 1): w < group_wide - 1,
        ("col", 0): n > 0,
        ("col", 1): n < group - 1,
    }

    order = [lax.rem(chip + by, chips) for by in range(1, chips)] + [chip]

    def own(device):
        return slots_ref.at[0, :, :, pl.ds(pl.multiple_of(device * breadth, LANES), breadth)]

    mine_loads = [
        pltpu.make_async_copy(own(order[step] * pair + core), mine.at[step], mine_sems.at[step])
        for step in range(chips)
    ]
    loads = [
        pltpu.make_async_copy(source, target, load_sems.at[i])
        for i, (source, target) in enumerate(
            [
                (owner_hbm, owner_ref),
                (class_hbm, class_ref),
                (speed_hbm, speed_ref),
                (row_velocity_hbm, row_velocity_ref),
                (column_velocity_hbm, column_velocity_ref),
                (sea_hbm, sea_ref),
                (final_hbm, final_ref),
                (deposit_hbm, deposit_ref),
            ]
        )
    ]
    barrier = pltpu.get_barrier_semaphore()
    for side in (0, 1):
        @pl.when(has["row", side])
        def _():
            pl.semaphore_signal(
                barrier, inc=1, device_id=(w + (2 * side - 1), n), device_id_type=MESH
            )
    for by in range(1, group):
        pl.semaphore_signal(
            barrier, inc=1, device_id=(w, lax.rem(n + by, group)), device_id_type=MESH
        )
    loads[0].start()
    for load in mine_loads:
        load.start()
    for load in loads[1:]:
        load.start()
    pads = jnp.zeros((ROWS, breadth), jnp.float32)
    bottom_pad = slice(height + ROWS, height + 2 * ROWS)
    for k in range(layers):
        grad[k, 0:ROWS, :] = pads
        grad[k, bottom_pad, :] = pads
    for t in range(4):
        wr[t, 0:ROWS, :] = pads
        wr[t, bottom_pad, :] = pads
    arrivals = (
        group - 1 + has["row", 0].astype(jnp.int32) + has["row", 1].astype(jnp.int32)
    )
    pl.semaphore_wait(barrier, arrivals)

    def near_copy(step):
        partner = chip * pair + (pair - 1 - core)
        target = order[step] * pair + (pair - 1 - core)
        return pltpu.make_async_remote_copy(
            src_ref=own(target),
            dst_ref=near.at[step],
            send_sem=near_sems.at[0, step],
            recv_sem=near_sems.at[1, step],
            device_id=(w, partner),
            device_id_type=MESH,
        )

    def far_copy(step, k):
        return pltpu.make_async_remote_copy(
            src_ref=mixed.at[step, k],
            dst_ref=far.at[step, k],
            send_sem=far_sems.at[0, step, k],
            recv_sem=far_sems.at[1, step, k],
            device_id=(w, order[step] * pair + core),
            device_id_type=MESH,
        )

    if pair == 2:
        for step in range(chips):
            near_copy(step).start()
    partner_slot = chip * pair + (pair - 1 - core)

    def chosen(step, k, rows):
        value = mine[step, k, rows, :]
        if pair == 2:
            value = jnp.where(owner_ref[k] == n, value, near[step, k, rows, :])
        return value

    loads[0].wait()
    for step in range(chips - 1):
        mine_loads[step].wait()
        if pair == 2:
            near_copy(step).wait_recv()
        for k in range(layers):
            for rows, _r in blocks:
                mixed[step, k, rows, :] = chosen(step, k, rows)
            far_copy(step, k).start()

    for load in loads[1:]:
        load.wait()
    speeds = []
    for k in range(layers):
        total = 0.0
        for c in range(speed_ref.shape[0]):
            total = jnp.where(class_ref[k] == c, speed_ref[c], total)
        speeds.append(total)

    for rows, r in blocks:
        inner = slice(ROWS + r, 2 * ROWS + r)
        row_w = stencil_weights(row_velocity_ref[rows, :])
        col_w = stencil_weights(column_velocity_ref[rows, :])
        for t, offset in enumerate(offsets):
            wr[t, inner, :] = row_w[offset + 2]
            wc[t, rows, :] = col_w[offset + 2]
        centre[rows, :] = 1.0 + row_w[2] + col_w[2]
        sea[rows, :] = sea_ref[rows, :].astype(jnp.float32)

    mine_loads[chips - 1].wait()
    if pair == 2:
        near_copy(chips - 1).wait_recv()
    for k in range(layers):
        for step in range(chips - 1):
            far_copy(step, k).wait_recv()
        for rows, r in blocks:
            value = chosen(chips - 1, k, rows)
            for step in range(chips - 1):
                sender = lax.rem(chip + chips - 1 - step, chips)
                value = jnp.where(
                    lax.div(owner_ref[k], pair) == sender, far[step, k, rows, :], value
                )
            field[0, k, ROWS + r : 2 * ROWS + r, :] = value

    def halo_copies(turn):
        copies = {}
        for side in (0, 1):
            by = 2 * side - 1
            copies["row", side] = pltpu.make_async_remote_copy(
                src_ref=row_send.at[turn, side],
                dst_ref=row_recv.at[turn, side],
                send_sem=halo_send_sems.at[turn, side],
                recv_sem=halo_recv_sems.at[turn, side],
                device_id=(w + by, n),
                device_id_type=MESH,
            )
            if turn < STEPS:
                edge = slice(0, LANES) if side == 0 else slice(breadth - LANES, breadth)
                source = field.at[turn, :, ROWS : ROWS + height, edge]
            else:
                source = col_send.at[turn - STEPS, side]
            copies["col", side] = pltpu.make_async_remote_copy(
                src_ref=source,
                dst_ref=col_recv.at[turn, side],
                send_sem=halo_send_sems.at[turn, 2 + side],
                recv_sem=halo_recv_sems.at[turn, 2 + side],
                device_id=(w, n + by),
                device_id_type=MESH,
            )
        return copies

    def send_halo(turn, which):
        for (kind, side), copy in halo_copies(turn).items():
            if kind == which:
                pl.when(has[kind, side])(copy.start)

    def send_field_rows(turn):
        for k in range(layers):
            rim = slice(k * RIM, (k + 1) * RIM)
            row_send[turn, 0, rim, :] = field[turn, k, ROWS : ROWS + RIM, :]
            row_send[turn, 1, rim, :] = field[turn, k, ROWS + height - RIM : ROWS + height, :]
        send_halo(turn, "row")

    def send_grad_rows(turn):
        for k in range(layers):
            rim = slice(k * RIM, (k + 1) * RIM)
            for side, signs, at in ((0, (0, 1), ROWS - RIM), (1, (2, 3), ROWS + height)):
                total = None
                for t in signs:
                    o = offsets[t]
                    spot = slice(at - o, at - o + RIM)
                    term = wr[t, spot, :] * grad[k, spot, :]
                    total = term if total is None else total + term
                row_send[turn, side, rim, :] = total
        send_halo(turn, "row")

    edges = blocks[:1] + blocks[1:][-1:]
    edges_first = edges + blocks[1:-1]

    def receive_halo(turn):
        for (kind, side), copy in halo_copies(turn).items():
            pl.when(has[kind, 1 - side])(copy.wait_recv)

    def ghost(side, kind):
        return has[kind, 1 - side]

    send_field_rows(0)
    for turn in range(STEPS):
        send_halo(turn, "col")
        receive_halo(turn)
        for k in range(layers):
            rim = slice(k * RIM, (k + 1) * RIM)
            field[turn, k, ROWS - RIM : ROWS, :] = jnp.where(
                ghost(1, "row"), row_recv[turn, 1, rim, :], 0.0
            )
            field[turn, k, ROWS + height : ROWS + height + RIM, :] = jnp.where(
                ghost(0, "row"), row_recv[turn, 0, rim, :], 0.0
            )
        for i, (rows, r) in enumerate(edges_first):
            above = None
            for k in range(layers):
                base = ROWS + r
                here = field[turn, k, base : base + ROWS, :]
                wide = jnp.concatenate(
                    [
                        jnp.where(ghost(1, "col"), col_recv[turn, 1, k, rows, :], 0.0),
                        here,
                        jnp.where(ghost(0, "col"), col_recv[turn, 0, k, rows, :], 0.0),
                    ],
                    axis=1,
                )
                adv = centre[rows, :] * here
                for t, o in enumerate(offsets):
                    adv += wr[t, base : base + ROWS, :] * field[turn, k, base + o : base + o + ROWS, :]
                    moved = pltpu.roll(wide, (-o) % wide.shape[1], 1)
                    adv += wc[t, rows, :] * moved[:, LANES : LANES + breadth]
                square = adv * adv
                part = 1.0 / (1.0 + square)
                slope[turn, k, rows, :] = speeds[k] * (1.0 - square) * part * part
                if turn + 1 < STEPS:
                    flux = speeds[k] * adv * part
                    left = adv - flux
                    if above is not None:
                        left = left + above
                    field[turn + 1, k, base : base + ROWS, :] = left * sea[rows, :]
                    above = flux
            if turn + 1 < STEPS and i + 1 == len(edges):
                send_field_rows(turn + 1)

    for turn in range(STEPS, 2 * STEPS):
        back = turn - STEPS
        step = STEPS - 1 - back
        adjoint = final_ref if back == 0 else out_ref
        for i, (rows, r) in enumerate(edges_first):
            base = ROWS + r
            mask = sea[rows, :]
            below = mask * deposit_ref[rows, :]
            for k in reversed(range(layers)):
                masked = adjoint[k, rows, :] * mask
                g = masked + (below - masked) * slope[step, k, rows, :]
                below = masked
                grad[k, base : base + ROWS, :] = g
                wall = jnp.zeros((ROWS, LANES), jnp.float32)
                gathered = None
                for t, o in enumerate(offsets):
                    product = jnp.concatenate([wall, wc[t, rows, :] * g, wall], axis=1)
                    moved = pltpu.roll(product, o % product.shape[1], 1)
                    gathered = moved if gathered is None else gathered + moved
                col_send[back, 0, k, rows, :] = gathered[:, :LANES]
                col_send[back, 1, k, rows, :] = gathered[:, LANES + breadth :]
                out_ref[k, rows, :] = gathered[:, LANES : LANES + breadth] + centre[rows, :] * g
            if i + 1 == len(edges):
                send_grad_rows(turn)
        send_halo(turn, "col")
        for k in range(layers):
            for rows, r in blocks:
                total = out_ref[k, rows, :]
                for t, o in enumerate(offsets):
                    spot = slice(ROWS + r - o, 2 * ROWS + r - o)
                    total += wr[t, spot, :] * grad[k, spot, :]
                out_ref[k, rows, :] = total
        receive_halo(turn)
        for k in range(layers):
            rim = slice(k * RIM, (k + 1) * RIM)
            out_ref[k, 0:RIM, :] += jnp.where(
                ghost(1, "row"), row_recv[turn, 1, rim, :], 0.0
            )
            out_ref[k, height - RIM : height, :] += jnp.where(
                ghost(0, "row"), row_recv[turn, 0, rim, :], 0.0
            )
            out_ref[k, :, 0:LANES] += jnp.where(
                ghost(1, "col"), col_recv[turn, 1, k], 0.0
            )
            out_ref[k, :, breadth - LANES : breadth] += jnp.where(
                ghost(0, "col"), col_recv[turn, 0, k], 0.0
            )

    if pair == 2:
        for step in range(chips):
            near_copy(step).wait_send()
    for step in range(chips - 1):
        for k in range(layers):
            far_copy(step, k).wait_send()
    for turn in range(2 * STEPS):
        for (kind, side), copy in halo_copies(turn).items():
            pl.when(has[kind, side])(copy.wait_send)


def body(group_wide, group, slots, owner, row_v, col_v, land_sea, layer_class, speed, final, deposit):
    layers, height, breadth = final.shape
    pair = 2 if group % 2 == 0 else 1
    chips = group // pair
    f32 = jnp.float32
    padded = height + 2 * ROWS
    vmem = pl.BlockSpec(memory_space=pltpu.VMEM)
    hbm = pl.BlockSpec(memory_space=pltpu.HBM)
    turns = 2 * STEPS
    return pl.pallas_call(
        functools.partial(kernel, group_wide, group),
        out_shape=jax.ShapeDtypeStruct(final.shape, f32),
        in_specs=[hbm] * 9,
        out_specs=vmem,
        scratch_shapes=[
            pltpu.SMEM(owner.shape, owner.dtype),
            pltpu.SMEM(layer_class.shape, layer_class.dtype),
            pltpu.SMEM(speed.shape, speed.dtype),
            pltpu.VMEM(row_v.shape, f32),
            pltpu.VMEM(col_v.shape, f32),
            pltpu.VMEM(land_sea.shape, land_sea.dtype),
            pltpu.VMEM(final.shape, f32),
            pltpu.VMEM(deposit.shape, f32),
            pltpu.VMEM((chips, layers, height, breadth), f32),
            pltpu.SemaphoreType.DMA((8,)),
            pltpu.SemaphoreType.DMA((chips,)),
            pltpu.VMEM((chips, layers, height, breadth), f32),
            pltpu.VMEM((max(chips - 1, 1), layers, height, breadth), f32),
            pltpu.VMEM((max(chips - 1, 1), layers, height, breadth), f32),
            pltpu.VMEM((STEPS, layers, padded, breadth), f32),
            pltpu.VMEM((STEPS, layers, height, breadth), f32),
            pltpu.VMEM((layers, padded, breadth), f32),
            pltpu.VMEM((4, padded, breadth), f32),
            pltpu.VMEM((4, height, breadth), f32),
            pltpu.VMEM((height, breadth), f32),
            pltpu.VMEM((height, breadth), f32),
            pltpu.VMEM((turns, 2, layers * RIM, breadth), f32),
            pltpu.VMEM((turns, 2, layers * RIM, breadth), f32),
            pltpu.VMEM((STEPS, 2, layers, height, LANES), f32),
            pltpu.VMEM((turns, 2, layers, height, LANES), f32),
            pltpu.SemaphoreType.DMA((2, chips)),
            pltpu.SemaphoreType.DMA((2, max(chips - 1, 1), layers)),
            pltpu.SemaphoreType.DMA((turns, 4)),
            pltpu.SemaphoreType.DMA((turns, 4)),
        ],
        compiler_params=pltpu.CompilerParams(
            collective_id=0, has_side_effects=True, vmem_limit_bytes=67043328
        ),
    )(owner, layer_class, speed, slots, row_v, col_v, land_sea, final, deposit)


def solution(mesh):
    in_specs = (
        P("narrow", None, "wide", None),
        P(),
        P("wide", "narrow"),
        P("wide", "narrow"),
        P("wide", "narrow"),
        P(),
        P(),
        P(None, "wide", "narrow"),
        P("wide", "narrow"),
    )
    out_specs = P(None, "wide", "narrow")
    return jax.shard_map(
        functools.partial(body, mesh.shape["wide"], mesh.shape["narrow"]),
        mesh=mesh,
        in_specs=in_specs,
        out_specs=out_specs,
        check_vma=False,
    )
```

profile of v0, /device:TPU:0, one launch (start us, length us, event | category | flops | bytes accessed | tf_op | source)
XLA Modules:
  0.0 36.4 jit_solution(3674778586512942910)
XLA Ops:
  0.0 34.7 %shard_map.91 = f32[2,32,1024]{2,1,0:T(8,128)} custom-call(s32[2]{0:T(128)} %owner_hbm.1, s32[2]{0:T(128)} %class_hbm.1, f32[4]{0:T(128)} %speed_hbm.1, f32[1,2,32,4096]{3,2,1,0:T(8,128)} %slots_ref.1, f32[32,1024]{1,0:T(8,128)} %row_velocity_hbm.1, f32[32,1024]{1,0:T(8,128)} %column_velocity_hbm.1, s32[32,1024]{1,0:T(8,128)} %sea_hbm.1, ...), custom_call_target="tpu_custom_call" | custom-call | tf_op jit(solution)/shard_map/pallas_call | solution.py:394
  34.7 1.7 %copy.11 = f32[2,32,1024]{2,1,0:T(8,128)} copy(f32[2,32,1024]{2,1,0:T(8,128)} %shard_map.91) | data formatting | bytes 524288
where the time goes:
time: 36.5 us; the launch traced here: 36.4 us
  Pallas kernels  34.7 us (95%)
  local copies, waits for them, and re-layouts  1.67 us (5%)
    pallas_call x1, Pallas kernels, body(): pl.pallas_call(functools.partial(kernel, group_wide, group), out_shape=ja...  34.7 us
    unnamed x1, local copies, waits for them, and re-layouts  1.67 us

commit v1 on v0

v1 whole, which is shorter than its diff:
```python
import functools

import jax
import jax.numpy as jnp
from jax import lax
from jax.experimental import pallas as pl
from jax.experimental.pallas import tpu as pltpu
from jax.sharding import PartitionSpec as P

STEPS = 3
LANES = 128
ROWS = 8
REACH = 2 * STEPS
OFFSETS = (-2, -1, 1, 2)
MESH = pl.DeviceIdType.MESH
VMEM_BYTES = 67043328


def stencil_weights(velocity):
    p = jnp.maximum(velocity, 0.0)
    q = jnp.minimum(velocity, 0.0)
    pp = p * p
    qq = q * q
    return [
        0.5 * pp - 0.5 * p,
        2.0 * p - pp,
        0.5 * pp - 1.5 * p + 0.5 * qq + 1.5 * q,
        -2.0 * q - qq,
        0.5 * qq + 0.5 * q,
    ]


def kernel(
    group_wide,
    group,
    owner_hbm,
    class_hbm,
    speed_hbm,
    slots_hbm,
    row_velocity_hbm,
    column_velocity_hbm,
    sea_hbm,
    final_hbm,
    deposit_hbm,
    out_ref,
    owner_ref,
    class_ref,
    speed_ref,
    sea_ref,
    fixed,
    fixed_col,
    given,
    given_col,
    mine,
    give,
    near,
    mixed,
    far,
    field,
    field_col,
    slope,
    grad,
    wr,
    wc,
    wr_back,
    wc_back,
    centre,
    round_send,
    round_recv,
    load_sems,
    slot_sems,
    near_sems,
    far_sems,
    fixed_sems,
    given_sems,
    col_sems,
    row_sems,
    corner_sems,
    round_sems,
):
    layers, height, breadth = out_ref.shape
    pair = 2
    chips = group // pair
    w = lax.axis_index("wide")
    n = lax.axis_index("narrow")
    chip = lax.div(n, pair)
    core = lax.rem(n, pair)
    width = breadth + LANES
    own_blocks = height // ROWS
    extended = height + 2 * ROWS
    all_blocks = list(range(own_blocks + 2))
    edge = (slice(0, LANES), slice(breadth - LANES, breadth))
    side_block = slice(breadth, width)
    own = slice(ROWS, ROWS + height)

    has_row = (w > 0, w < group_wide - 1)
    has_col = (n > 0, n < group - 1)
    row_device = ((w - 1, n), (w + 1, n))
    col_device = ((w, n - 1), (w, n + 1))
    partner = (w, chip * pair + (pair - 1 - core))
    order = [lax.rem(chip + by, chips) for by in range(1, chips)] + [chip]
    parts = (
        slice(0, ROWS),
        slice(height - ROWS, height),
        slice(ROWS, height - ROWS),
    )

    def columns_of(device):
        return pl.ds(pl.multiple_of(device * breadth, LANES), breadth)

    def remote(src, dst, send_sem, recv_sem, device):
        return pltpu.make_async_remote_copy(
            src_ref=src,
            dst_ref=dst,
            send_sem=send_sem,
            recv_sem=recv_sem,
            device_id=device,
            device_id_type=MESH,
        )

    small = [
        pltpu.make_async_copy(source, target, load_sems.at[i])
        for i, (source, target) in enumerate(
            [
                (owner_hbm, owner_ref),
                (class_hbm, class_ref),
                (speed_hbm, speed_ref),
                (sea_hbm, sea_ref),
                (row_velocity_hbm, fixed.at[0, own, 0:breadth]),
                (column_velocity_hbm, fixed.at[1, own, 0:breadth]),
                (final_hbm, given.at[0:layers, own, 0:breadth]),
                (deposit_hbm, given.at[layers, own, 0:breadth]),
            ]
        )
    ]
    give_loads = [
        pltpu.make_async_copy(
            slots_hbm.at[0, :, :, columns_of(order[step] * pair + (pair - 1 - core))],
            give.at[step],
            slot_sems.at[0, step],
        )
        for step in range(chips)
    ]
    mine_loads = [
        pltpu.make_async_copy(
            slots_hbm.at[0, :, :, columns_of(order[step] * pair + core)],
            mine.at[step],
            slot_sems.at[1, step],
        )
        for step in range(chips)
    ]

    barrier = pltpu.get_barrier_semaphore()
    for side in (0, 1):
        @pl.when(has_row[side])
        def _():
            pl.semaphore_signal(barrier, inc=1, device_id=row_device[side], device_id_type=MESH)
    for by in range(1, group):
        pl.semaphore_signal(
            barrier, inc=1, device_id=(w, lax.rem(n + by, group)), device_id_type=MESH
        )
    for load in give_loads[:1] + mine_loads[:1] + small + give_loads[1:] + mine_loads[1:]:
        load.start()

    halo_rows = (slice(0, ROWS), slice(ROWS + height, extended))
    zeros = jnp.zeros((ROWS, width), jnp.float32)
    for side in (0, 1):
        @pl.when(jnp.logical_not(has_row[side]))
        def _():
            for i in range(3):
                fixed[i, halo_rows[side], :] = zeros
            given[layers, halo_rows[side], :] = zeros
            inner = slice(ROWS + halo_rows[side].start, ROWS + halo_rows[side].stop)
            for k in range(layers):
                field[0, k, inner, :] = zeros
                grad[STEPS - 1, k, inner, :] = zeros

        @pl.when(jnp.logical_not(has_col[side]))
        def _():
            for i in range(3):
                fixed_col[side, i] = jnp.zeros((height, LANES), jnp.float32)
            for i in range(layers + 1):
                given_col[side, i] = jnp.zeros((height, LANES), jnp.float32)
            for k in range(layers):
                field_col[side, k] = jnp.zeros((height, LANES), jnp.float32)

    for past in (slice(0, ROWS), slice(extended + ROWS, extended + 2 * ROWS)):
        for step in range(STEPS):
            for k in range(layers):
                field[step, k, past, :] = zeros
                grad[step, k, past, :] = zeros
        for t in range(4):
            wr[t, past, :] = zeros

    small[3].wait()
    for r in range(0, height, ROWS):
        fixed[2, ROWS + r : 2 * ROWS + r, 0:breadth] = sea_ref[r : r + ROWS, :].astype(jnp.float32)
    small[4].wait()
    small[5].wait()

    arrivals = group - 1 + has_row[0].astype(jnp.int32) + has_row[1].astype(jnp.int32)
    pl.semaphore_wait(barrier, arrivals)

    def near_copy(step, i):
        return remote(
            give.at[step, :, parts[i], :],
            near.at[step, :, parts[i], :],
            near_sems.at[0, step, i],
            near_sems.at[1, step, i],
            partner,
        )

    def far_copy(step, name):
        kind, a, b = name
        if kind == "edge":
            spot = (slice(None), parts[a], edge[b])
        elif kind == "inner":
            spot = (a, parts[b], slice(LANES, breadth - LANES))
        else:
            spot = (slice(None), parts[2], slice(LANES, breadth - LANES))
        at = far_names.index(name)
        return remote(
            mixed.at[(step, *spot)],
            far.at[(step, *spot)],
            far_sems.at[0, step, at],
            far_sems.at[1, step, at],
            (w, order[step] * pair + core),
        )

    far_names = (
        [("edge", i, side) for i in (0, 1) for side in (0, 1)]
        + [("inner", k, i) for k in range(layers) for i in (0, 1)]
        + [("edge", 2, side) for side in (0, 1)]
        + [("middle", 0, 0)]
    )

    give_loads[0].wait()
    for step in range(chips):
        if step:
            give_loads[step].wait()
        for i in range(3):
            near_copy(step, i).start()

    def fixed_row(side):
        source = halo_rows[side].start + (ROWS if side == 0 else -ROWS)
        return remote(
            fixed.at[:, source : source + ROWS, 0:breadth],
            fixed.at[:, halo_rows[1 - side], 0:breadth],
            fixed_sems.at[0, 0, side],
            fixed_sems.at[1, 0, 1 - side],
            row_device[side],
        )

    def fixed_column(side):
        return remote(
            fixed.at[:, own, edge[side]],
            fixed_col.at[1 - side],
            fixed_sems.at[0, 1, side],
            fixed_sems.at[1, 1, 1 - side],
            col_device[side],
        )

    def fixed_corner(side):
        source = halo_rows[side].start + (ROWS if side == 0 else -ROWS)
        return remote(
            fixed.at[:, source : source + ROWS, side_block],
            fixed.at[:, halo_rows[1 - side], side_block],
            fixed_sems.at[0, 2, side],
            fixed_sems.at[1, 2, 1 - side],
            row_device[side],
        )

    def given_column(side):
        return remote(
            given.at[:, own, edge[side]],
            given_col.at[1 - side],
            given_sems.at[0, 0, side],
            given_sems.at[1, 0, 1 - side],
            col_device[side],
        )

    def given_row(side):
        source = halo_rows[side].start + (ROWS if side == 0 else -ROWS)
        return remote(
            given.at[layers, source : source + ROWS, :],
            given.at[layers, halo_rows[1 - side], :],
            given_sems.at[0, 1, side],
            given_sems.at[1, 1, 1 - side],
            row_device[side],
        )

    def start(has, *makers):
        for side in (0, 1):
            @pl.when(has[side])
            def _():
                for maker in makers:
                    maker(side).start()

    def arrived(has, *makers):
        for side in (0, 1):
            @pl.when(has[side])
            def _():
                for maker in makers:
                    maker(1 - side).wait_recv()

    start(has_col, fixed_column)
    start(has_row, fixed_row)

    small[0].wait()

    def mix(step, k, rows, lanes):
        mixed[step, k, rows, lanes] = jnp.where(
            owner_ref[k] == n, mine[step, k, rows, lanes], near[step, k, rows, lanes]
        )

    def blocks_of(rows):
        return [slice(r, r + ROWS) for r in range(rows.start, rows.stop, ROWS)]

    everything = slice(0, breadth)
    for step in range(chips - 1):
        mine_loads[step].wait()
        for i in (0, 1):
            near_copy(step, i).wait_recv()
            for k in range(layers):
                mix(step, k, parts[i], everything)
            for side in (0, 1):
                far_copy(step, ("edge", i, side)).start()
        for k in range(layers):
            for i in (0, 1):
                far_copy(step, ("inner", k, i)).start()
        near_copy(step, 2).wait_recv()
        for k in range(layers):
            for rows in blocks_of(parts[2]):
                mix(step, k, rows, everything)
        for side in (0, 1):
            far_copy(step, ("edge", 2, side)).start()
        far_copy(step, ("middle", 0, 0)).start()

    last = chips - 1
    mine_loads[last].wait()
    for i in range(3):
        near_copy(last, i).wait_recv()

    small[1].wait()
    small[2].wait()
    speeds = []
    for k in range(layers):
        total = 0.0
        for c in range(speed_ref.shape[0]):
            total = jnp.where(class_ref[k] == c, speed_ref[c], total)
        speeds.append(total)

    def join(right, left):
        lane = lax.broadcasted_iota(jnp.int32, right.shape, right.ndim - 1)
        return jnp.where(lane < LANES // 2, right, left)

    arrived(has_col, fixed_column)
    for i in range(3):
        for r in range(0, height, ROWS):
            rows = slice(r, r + ROWS)
            fixed[i, ROWS + r : 2 * ROWS + r, side_block] = join(
                fixed_col[1, i, rows, :], fixed_col[0, i, rows, :]
            )
    start(has_row, fixed_corner)

    def make_weights(b):
        rows = slice(b * ROWS, (b + 1) * ROWS)
        inner = slice((b + 1) * ROWS, (b + 2) * ROWS)
        row_w = stencil_weights(fixed[0, rows, :])
        col_w = stencil_weights(fixed[1, rows, :])
        for t, offset in enumerate(OFFSETS):
            wr[t, inner, :] = row_w[offset + 2]
            wc[t, rows, :] = col_w[offset + 2]
            wc_back[3 - t, rows, :] = pltpu.roll(col_w[offset + 2], offset % width, 1)
        centre[rows, :] = 1.0 + row_w[2] + col_w[2]

    def turn_weights(b):
        for t, offset in enumerate(OFFSETS):
            base = (b + 1) * ROWS + offset
            wr_back[t, b * ROWS : (b + 1) * ROWS, :] = wr[3 - t, base : base + ROWS, :]

    for b in all_blocks[1:-1]:
        make_weights(b)

    small[6].wait()
    small[7].wait()
    start(has_col, given_column)

    def chosen(k, rows, lanes):
        value = jnp.where(
            owner_ref[k] == n, mine[last, k, rows, lanes], near[last, k, rows, lanes]
        )
        for step in range(chips - 1):
            sender = lax.rem(chip + chips - 1 - step, chips)
            value = jnp.where(
                lax.div(owner_ref[k], pair) == sender, far[step, k, rows, lanes], value
            )
        return value

    def put(k, rows, lanes):
        for piece in blocks_of(rows):
            spot = slice(2 * ROWS + piece.start, 2 * ROWS + piece.stop)
            field[0, k, spot, lanes] = chosen(k, piece, lanes)

    def shifted(rows):
        return slice(2 * ROWS + rows.start, 2 * ROWS + rows.stop)

    def field_column(i):
        def make(side):
            return remote(
                field.at[0, :, shifted(parts[i]), edge[side]],
                field_col.at[1 - side, :, parts[i], :],
                col_sems.at[0, i, side],
                col_sems.at[1, i, 1 - side],
                col_device[side],
            )

        return make

    wide_halo = (slice(ROWS, 2 * ROWS), slice(2 * ROWS + height, 3 * ROWS + height))

    def field_row(k):
        def make(side):
            return remote(
                field.at[0, k, shifted(parts[side]), 0:breadth],
                field.at[0, k, wide_halo[1 - side], 0:breadth],
                row_sems.at[0, k, side],
                row_sems.at[1, k, 1 - side],
                row_device[side],
            )

        return make

    def field_corner(side):
        return remote(
            field.at[0, :, shifted(parts[side]), side_block],
            field.at[0, :, wide_halo[1 - side], side_block],
            corner_sems.at[0, side],
            corner_sems.at[1, 1 - side],
            row_device[side],
        )

    def take(name):
        for step in range(chips - 1):
            far_copy(step, name).wait_recv()

    for i in (0, 1):
        for side in (0, 1):
            take(("edge", i, side))
            for k in range(layers):
                put(k, parts[i], edge[side])
        start(has_col, field_column(i))
    for k in range(layers):
        for i in (0, 1):
            take(("inner", k, i))
            put(k, parts[i], slice(LANES, breadth - LANES))

            @pl.when(has_row[i])
            def _():
                field_row(k)(i).start()
    for side in (0, 1):
        take(("edge", 2, side))
        for k in range(layers):
            put(k, parts[2], edge[side])
    start(has_col, field_column(2))

    def join_field(rows):
        for k in range(layers):
            for piece in blocks_of(rows):
                field[0, k, shifted(piece), side_block] = join(
                    field_col[1, k, piece, :], field_col[0, k, piece, :]
                )

    for i in (0, 1):
        arrived(has_col, field_column(i))
        join_field(parts[i])

        @pl.when(has_row[i])
        def _():
            field_corner(i).start()

    arrived(has_col, given_column)
    for i in range(layers + 1):
        for r in range(0, height, ROWS):
            rows = slice(r, r + ROWS)
            given[i, ROWS + r : 2 * ROWS + r, side_block] = join(
                given_col[1, i, rows, :], given_col[0, i, rows, :]
            )
    start(has_row, given_row)

    take(("middle", 0, 0))
    for k in range(layers):
        put(k, parts[2], slice(LANES, breadth - LANES))

    arrived(has_row, fixed_row, fixed_corner)
    make_weights(0)
    make_weights(all_blocks[-1])
    for b in all_blocks:
        turn_weights(b)

    arrived(has_col, field_column(2))
    join_field(parts[2])
    arrived(has_row, *[field_row(k) for k in range(layers)], field_corner)

    def stencil(source, b, rows_w, cols_w):
        base = (b + 1) * ROWS
        rows = slice(b * ROWS, (b + 1) * ROWS)
        here = source[base : base + ROWS, :]
        total = centre[rows, :] * here
        for t, o in enumerate(OFFSETS):
            total += rows_w[t] * source[base + o : base + o + ROWS, :]
            total += cols_w[t] * pltpu.roll(here, (-o) % width, 1)
        return total

    def forward(step, b):
        rows = slice(b * ROWS, (b + 1) * ROWS)
        inner = slice((b + 1) * ROWS, (b + 2) * ROWS)
        rows_w = [wr[t, inner, :] for t in range(4)]
        cols_w = [wc[t, rows, :] for t in range(4)]
        above = None
        for k in range(layers):
            adv = stencil(field.at[step, k], b, rows_w, cols_w)
            square = adv * adv
            part = 1.0 / (1.0 + square)
            slope[step, k, rows, :] = speeds[k] * (1.0 - square) * part * part
            if step + 1 < STEPS:
                flux = speeds[k] * adv * part
                left = adv - flux
                if above is not None:
                    left = left + above
                field[step + 1, k, inner, :] = left * fixed[2, rows, :]
                above = flux

    def settle_back(step, b, adjoint):
        rows = slice(b * ROWS, (b + 1) * ROWS)
        inner = slice((b + 1) * ROWS, (b + 2) * ROWS)
        mask = fixed[2, rows, :]
        below = mask * given[layers, rows, :]
        for k in reversed(range(layers)):
            masked = adjoint[k] * mask
            grad[step, k, inner, :] = masked + (below - masked) * slope[step, k, rows, :]
            below = masked

    def back(step, b):
        rows = slice(b * ROWS, (b + 1) * ROWS)
        rows_w = [wr_back[t, rows, :] for t in range(4)]
        cols_w = [wc_back[t, rows, :] for t in range(4)]
        adjoint = [stencil(grad.at[step, k], b, rows_w, cols_w) for k in range(layers)]
        if step:
            settle_back(step - 1, b, adjoint)
        else:
            spot = slice((b - 1) * ROWS, b * ROWS)
            for k in range(layers):
                out_ref[k, spot, :] = adjoint[k][:, 0:breadth]

    final_step = STEPS - 1

    def last_forward(b):
        forward(final_step, b)
        rows = slice(b * ROWS, (b + 1) * ROWS)
        settle_back(final_step, b, [given[k, rows, :] for k in range(layers)])

    quad = round_send.shape[2]

    def pieces():
        for k in range(layers):
            r = 0
            while r < REACH:
                at = k * REACH + r
                count = min(REACH - r, quad - at % quad)
                yield k, r, count, at // quad, at % quad
                r += count

    def round_copy(side):
        return remote(
            round_send.at[side],
            round_recv.at[1 - side],
            round_sems.at[0, side],
            round_sems.at[1, 1 - side],
            row_device[side],
        )

    def send_round(side):
        first = 2 * ROWS if side == 0 else 2 * ROWS + height - REACH
        for k, r, count, j, at in pieces():
            round_send[side, j, at : at + count, :] = grad[
                final_step, k, first + r : first + r + count, :
            ]

        @pl.when(has_row[side])
        def _():
            round_copy(side).start()

    def receive_round(side):
        first = 2 * ROWS - REACH if side == 0 else 2 * ROWS + height

        @pl.when(has_row[side])
        def _():
            round_copy(1 - side).wait_recv()
            for k, r, count, j, at in pieces():
                grad[final_step, k, first + r : first + r + count, :] = round_recv[
                    side, j, at : at + count, :
                ]

    for step in range(final_step):
        for b in all_blocks:
            forward(step, b)
    last_forward(1)
    send_round(0)
    last_forward(own_blocks)
    send_round(1)
    inside = all_blocks[2:-2]
    for b in inside:
        last_forward(b)

    for step in range(final_step, 0, -1):
        for b in all_blocks[1:-1]:
            back(step, b)
    for b in inside:
        back(0, b)

    arrived(has_row, given_row)
    outside = (all_blocks[:2], all_blocks[-2:])
    for side in (0, 1):
        receive_round(side)
        for step in range(final_step, 0, -1):
            for b in outside[side]:
                back(step, b)
    back(0, 1)
    back(0, own_blocks)

    def left(has, *makers):
        for side in (0, 1):
            @pl.when(has[side])
            def _():
                for maker in makers:
                    maker(side).wait_send()

    for step in range(chips):
        for i in range(3):
            near_copy(step, i).wait_send()
    for step in range(chips - 1):
        for name in far_names:
            far_copy(step, name).wait_send()
    left(has_col, fixed_column, given_column, *[field_column(i) for i in range(3)])
    left(
        has_row,
        fixed_row,
        fixed_corner,
        given_row,
        *[field_row(k) for k in range(layers)],
        field_corner,
        round_copy,
    )


def body(group_wide, group, slots, owner, row_v, col_v, land_sea, layer_class, speed, final, deposit):
    layers, height, breadth = final.shape
    chips = group // 2
    hops = max(chips - 1, 1)
    f32 = jnp.float32
    extended = height + 2 * ROWS
    padded = extended + 2 * ROWS
    width = breadth + LANES
    quads = layers * REACH // 4
    dma = pltpu.SemaphoreType.DMA
    vmem = pl.BlockSpec(memory_space=pltpu.VMEM)
    hbm = pl.BlockSpec(memory_space=pltpu.HBM)
    return pl.pallas_call(
        functools.partial(kernel, group_wide, group),
        out_shape=pltpu.VMEM(final.shape, f32),
        in_specs=[hbm] * 9,
        out_specs=vmem,
        scratch_shapes=[
            pltpu.SMEM(owner.shape, owner.dtype),
            pltpu.SMEM(layer_class.shape, layer_class.dtype),
            pltpu.SMEM(speed.shape, speed.dtype),
            pltpu.VMEM(land_sea.shape, land_sea.dtype),
            pltpu.VMEM((3, extended, width), f32),
            pltpu.VMEM((2, 3, height, LANES), f32),
            pltpu.VMEM((layers + 1, extended, width), f32),
            pltpu.VMEM((2, layers + 1, height, LANES), f32),
            pltpu.VMEM((chips, layers, height, breadth), f32),
            pltpu.VMEM((chips, layers, height, breadth), f32),
            pltpu.VMEM((chips, layers, height, breadth), f32),
            pltpu.VMEM((hops, layers, height, breadth), f32),
            pltpu.VMEM((hops, layers, height, breadth), f32),
            pltpu.VMEM((STEPS, layers, padded, width), f32),
            pltpu.VMEM((2, layers, height, LANES), f32),
            pltpu.VMEM((STEPS, layers, extended, width), f32),
            pltpu.VMEM((STEPS, layers, padded, width), f32),
            pltpu.VMEM((4, padded, width), f32),
            pltpu.VMEM((4, extended, width), f32),
            pltpu.VMEM((4, extended, width), f32),
            pltpu.VMEM((4, extended, width), f32),
            pltpu.VMEM((extended, width), f32),
            pltpu.VMEM((2, quads, 4, width), f32),
            pltpu.VMEM((2, quads, 4, width), f32),
            dma((8,)),
            dma((2, chips)),
            dma((2, chips, 3)),
            dma((2, hops, 7 + 2 * layers)),
            dma((2, 3, 2)),
            dma((2, 2, 2)),
            dma((2, 3, 2)),
            dma((2, layers, 2)),
            dma((2, 2)),
            dma((2, 2)),
        ],
        compiler_params=pltpu.CompilerParams(
            collective_id=0,
            has_side_effects=True,
            vmem_limit_bytes=VMEM_BYTES - final.size * final.dtype.itemsize,
        ),
    )(owner, layer_class, speed, slots, row_v, col_v, land_sea, final, deposit)


def solution(mesh):
    in_specs = (
        P("narrow", None, "wide", None),
        P(),
        P("wide", "narrow"),
        P("wide", "narrow"),
        P("wide", "narrow"),
        P(),
        P(),
        P(None, "wide", "narrow"),
        P("wide", "narrow"),
    )
    out_specs = P(None, "wide", "narrow")
    return jax.shard_map(
        functools.partial(body, mesh.shape["wide"], mesh.shape["narrow"]),
        mesh=mesh,
        in_specs=in_specs,
        out_specs=out_specs,
        check_vma=False,
    )
```

time: 36.5 us -> 21.6 us (0.59)
  the two profiles are of different devices: /device:TPU:0 before, /device:TPU:10 now
where the time goes in v1:
time: 21.6 us; the launch traced here: 21.5 us
  Pallas kernels  20.8 us (96%)
  local copies, waits for them, and re-layouts  0.71 us (3%)
    pallas_call x1, Pallas kernels, body(): pl.pallas_call(functools.partial(kernel, group_wide, group), out_shape=pl...  20.8 us
    unnamed x1, local copies, waits for them, and re-layouts  0.71 us

profile of v1, /device:TPU:10, one launch (start us, length us, event | category | flops | bytes accessed | tf_op | source)
XLA Modules:
  0.0 21.5 jit_solution(10062188632340185209)
XLA Ops:
  0.0 20.8 %shard_map.91 = f32[2,32,1024]{2,1,0:T(8,128)S(1)} custom-call(s32[2]{0:T(128)} %owner_hbm.1, s32[2]{0:T(128)} %class_hbm.1, f32[4]{0:T(128)} %speed_hbm.1, f32[1,2,32,4096]{3,2,1,0:T(8,128)} %slots_hbm.1, f32[32,1024]{1,0:T(8,128)} %row_velocity_hbm.1, f32[32,1024]{1,0:T(8,128)} %column_velocity_hbm.1, s32[32,1024]{1,0:T(8,128)} %sea_hbm.1, ...), custom_call_target="tpu_custom_call" | custom-call | tf_op jit(solution)/shard_map/pallas_call | solution.py:669
  20.8 0.7 %copy.11 = f32[2,32,1024]{2,1,0:T(8,128)} copy(f32[2,32,1024]{2,1,0:T(8,128)S(1)} %shard_map.91) | data formatting | bytes 524288

commit v2 on v1

v2 whole, which is shorter than its diff:
```python
import functools

import jax
import jax.numpy as jnp
from jax import lax
from jax.experimental import pallas as pl
from jax.experimental.pallas import tpu as pltpu
from jax.sharding import PartitionSpec as P

STEPS = 3
LANES = 128
ROWS = 8
HALF = ROWS // 2
SHARE = 16
OFFSETS = (-2, -1, 1, 2)
MESH = pl.DeviceIdType.MESH
VMEM_BYTES = 67043328


def stencil_weights(velocity):
    p = jnp.maximum(velocity, 0.0)
    q = jnp.minimum(velocity, 0.0)
    pp = p * p
    qq = q * q
    return [
        0.5 * pp - 0.5 * p,
        2.0 * p - pp,
        0.5 * pp - 1.5 * p + 0.5 * qq + 1.5 * q,
        -2.0 * q - qq,
        0.5 * qq + 0.5 * q,
    ]


def kernel(
    group_wide,
    group,
    owner_hbm,
    class_hbm,
    speed_hbm,
    slots_hbm,
    row_velocity_hbm,
    column_velocity_hbm,
    sea_hbm,
    final_hbm,
    deposit_hbm,
    out_ref,
    owner_ref,
    class_ref,
    speed_ref,
    sea_ref,
    fixed,
    fixed_inner,
    given,
    given_inner,
    outer_send,
    outer_recv,
    mine,
    give,
    near,
    mixed,
    far,
    field,
    field_inner,
    field_outer,
    field_late,
    slope,
    grad,
    wr,
    wc,
    wr_back,
    wc_back,
    centre,
    round_send,
    round_recv,
    load_sems,
    slot_sems,
    near_sems,
    far_sems,
    fixed_sems,
    given_sems,
    col_sems,
    row_sems,
    corner_sems,
    late_sems,
    round_sems,
):
    layers, height, breadth = out_ref.shape
    pair = 2
    chips = group // pair
    w = lax.axis_index("wide")
    n = lax.axis_index("narrow")
    chip = lax.div(n, pair)
    core = lax.rem(n, pair)
    width = breadth + LANES
    own_blocks = height // ROWS
    extended = height + 2 * ROWS
    all_blocks = list(range(own_blocks + 2))
    inside = all_blocks[2:-2]
    edge = (slice(0, LANES), slice(breadth - LANES, breadth))
    side_block = slice(breadth, width)
    own = slice(ROWS, ROWS + height)

    has_row = (w > 0, w < group_wide - 1)
    row_device = ((w - 1, n), (w + 1, n))
    partner = (w, chip * pair + (pair - 1 - core))
    order = [lax.rem(chip + by, chips) for by in range(1, chips)] + [chip]
    parts = (
        slice(0, ROWS),
        slice(height - ROWS, height),
        slice(ROWS, height - ROWS),
    )
    def pieces_at(first, last):
        return (slice(first, last), slice(height - last, height - first))

    rim = pieces_at(0, HALF)
    second = pieces_at(HALF, 2 * HALF)
    third = pieces_at(2 * HALF, 3 * HALF)
    inward = pieces_at(HALF, 3 * HALF)
    core_rows = slice(3 * HALF, height - 3 * HALF)

    def columns_of(device):
        return pl.ds(pl.multiple_of(device * breadth, LANES), breadth)

    def outer_columns(device, at_core):
        start = device * breadth - LANES + at_core * (breadth + LANES)
        return pl.ds(pl.multiple_of(lax.rem(start + group * breadth, group * breadth), LANES), LANES)

    def has_outer(device):
        beside = device - 1 + 2 * core
        return jnp.logical_and(beside >= 0, beside < group)

    def remote(src, dst, send_sem, recv_sem, device):
        return pltpu.make_async_remote_copy(
            src_ref=src,
            dst_ref=dst,
            send_sem=send_sem,
            recv_sem=recv_sem,
            device_id=device,
            device_id_type=MESH,
        )

    small = [
        pltpu.make_async_copy(source, target, load_sems.at[i])
        for i, (source, target) in enumerate(
            [
                (owner_hbm, owner_ref),
                (class_hbm, class_ref),
                (speed_hbm, speed_ref),
                (sea_hbm, sea_ref),
                (row_velocity_hbm, fixed.at[0, own, 0:breadth]),
                (column_velocity_hbm, fixed.at[1, own, 0:breadth]),
                (final_hbm, given.at[0:layers, own, 0:breadth]),
                (deposit_hbm, given.at[layers, own, 0:breadth]),
            ]
        )
    ]
    def slot_loads(target, row, at_core):
        return [
            [
                pltpu.make_async_copy(
                    slots_hbm.at[0, :, :, columns(order[step] * pair + at_core)],
                    target.at[step, :, :, lanes],
                    slot_sems.at[row, i, step],
                )
                for i, (columns, lanes) in enumerate(
                    [
                        (columns_of, slice(0, breadth)),
                        (functools.partial(outer_columns, at_core=at_core), side_block),
                    ]
                )
            ]
            for step in range(chips)
        ]

    give_loads = slot_loads(give, 0, pair - 1 - core)
    mine_loads = slot_loads(mine, 1, core)

    halo_rows = (slice(0, ROWS), slice(ROWS + height, extended))
    barrier = pltpu.get_barrier_semaphore()
    for side in (0, 1):
        @pl.when(has_row[side])
        def _():
            pl.semaphore_signal(barrier, inc=1, device_id=row_device[side], device_id_type=MESH)
    for by in range(1, group):
        pl.semaphore_signal(
            barrier, inc=1, device_id=(w, lax.rem(n + by, group)), device_id_type=MESH
        )
    for load in give_loads[0] + mine_loads[0] + small + sum(give_loads[1:] + mine_loads[1:], []):
        load.start()

    arrivals = group - 1 + has_row[0].astype(jnp.int32) + has_row[1].astype(jnp.int32)
    pl.semaphore_wait(barrier, arrivals)

    def near_copy(step, i):
        return remote(
            give.at[step, :, parts[i], :],
            near.at[step, :, parts[i], :],
            near_sems.at[step, 3],
            near_sems.at[step, i],
            partner,
        )

    def far_copy(step, name):
        kind, rows, side = name
        if kind == "edge":
            lanes = edge[side]
        elif kind == "outer":
            lanes = side_block
        else:
            lanes = slice(LANES, breadth - LANES)
        spot = (slice(None), rows, lanes)
        at = far_names.index(name)
        return remote(
            mixed.at[(step, *spot)],
            far.at[(step, *spot)],
            far_sems.at[step, len(far_names) + int(kind == "outer")],
            far_sems.at[step, at],
            (w, order[step] * pair + core),
        )

    def rims_of(rows):
        return [("edge", rows, 0), ("edge", rows, 1), ("outer", rows, 0)]

    def main_of(rows):
        return ("main", rows, 0)

    far_names = []
    for i in (0, 1):
        far_names += rims_of(rim[i])
    far_names += [main_of(rim[i]) for i in (0, 1)]
    early = len(far_names)
    for i in (0, 1):
        far_names += rims_of(inward[i])
    far_names += [main_of(second[i]) for i in (0, 1)]
    far_names += rims_of(core_rows)
    far_names += [main_of(third[i]) for i in (0, 1)]
    far_names += [main_of(core_rows)]

    def far_start(step, name):
        if name[0] == "outer":
            pl.when(has_outer(order[step] * pair + core))(far_copy(step, name).start)
        else:
            far_copy(step, name).start()

    for step in range(chips):
        for load in give_loads[step]:
            load.wait()
        for i in range(3):
            near_copy(step, i).start()

    inner_edge = pl.ds(pl.multiple_of((1 - core) * (breadth - LANES), LANES), LANES)
    outer_edge = pl.ds(pl.multiple_of(core * (breadth - LANES), LANES), LANES)
    def near_edge(side, first, last):
        if side == 0:
            return slice(ROWS + first, ROWS + last), slice(
                ROWS + height + first, ROWS + height + last
            )
        return slice(ROWS + height - last, ROWS + height - first), slice(ROWS - last, ROWS - first)

    def fixed_row(side):
        source, target = near_edge(side, 0, ROWS - 2)
        return remote(
            fixed.at[:, source, 0:breadth],
            fixed.at[:, target, 0:breadth],
            fixed_sems.at[0, 0, side],
            fixed_sems.at[1, 0, 1 - side],
            row_device[side],
        )

    def fixed_column():
        return remote(
            fixed.at[:, own, inner_edge],
            fixed_inner,
            fixed_sems.at[0, 1, 0],
            fixed_sems.at[1, 1, 0],
            partner,
        )

    def given_column():
        return remote(
            given.at[:, own, inner_edge],
            given_inner,
            given_sems.at[0, 0, 0],
            given_sems.at[1, 0, 0],
            partner,
        )

    def outer_column():
        return remote(
            outer_send,
            outer_recv,
            fixed_sems.at[0, 1, 1],
            fixed_sems.at[1, 1, 1],
            (w, n - 1 + 2 * core),
        )

    def fixed_corner(side):
        source, target = near_edge(side, 0, ROWS - 2)
        return remote(
            fixed.at[:, source, side_block],
            fixed.at[:, target, side_block],
            fixed_sems.at[0, 2, side],
            fixed_sems.at[1, 2, 1 - side],
            row_device[side],
        )

    def given_row(side):
        source, target = near_edge(side, 0, 2 * (STEPS - 1))
        return remote(
            given.at[layers, source, :],
            given.at[layers, target, :],
            given_sems.at[0, 1, side],
            given_sems.at[1, 1, 1 - side],
            row_device[side],
        )

    def final_row(side):
        source, target = near_edge(side, 0, 2)
        return remote(
            given.at[0:layers, source, :],
            given.at[0:layers, target, :],
            given_sems.at[0, 2, side],
            given_sems.at[1, 2, 1 - side],
            row_device[side],
        )

    def start(has, *makers):
        for side in (0, 1):
            @pl.when(has[side])
            def _():
                for maker in makers:
                    maker(side).start()

    def arrived(has, *makers):
        for side in (0, 1):
            @pl.when(has[side])
            def _():
                for maker in makers:
                    maker(1 - side).wait_recv()

    small[3].wait()
    for r in range(0, height, ROWS):
        fixed[2, ROWS + r : 2 * ROWS + r, 0:breadth] = sea_ref[r : r + ROWS, :].astype(jnp.float32)
    small[4].wait()
    small[5].wait()

    start(has_row, fixed_row)
    fixed_column().start()
    small[6].wait()
    small[7].wait()
    given_column().start()
    shared = [(fixed, i) for i in range(3)] + [(given, i) for i in range(layers + 1)]
    lane = lax.broadcasted_iota(jnp.int32, (ROWS, LANES), 1)
    for r in range(0, height, ROWS):
        packed = jnp.zeros((ROWS, LANES), jnp.float32)
        for a, (ref, i) in enumerate(shared):
            moved = pltpu.roll(ref[i, ROWS + r : 2 * ROWS + r, outer_edge], SHARE * (a + core), 1)
            mine_lanes = jnp.logical_and(lane >= SHARE * a, lane < SHARE * (a + 1))
            packed = jnp.where(mine_lanes, moved, packed)
        outer_send[r : r + ROWS, :] = packed
    pl.when(has_outer(n))(outer_column().start)

    small[0].wait()

    def mix(step, k, rows, lanes):
        mixed[step, k, rows, lanes] = jnp.where(
            owner_ref[k] == n, mine[step, k, rows, lanes], near[step, k, rows, lanes]
        )

    def blocks_of(rows):
        return [slice(r, r + ROWS) for r in range(rows.start, rows.stop, ROWS)]

    everything = slice(0, width)
    for step in range(chips - 1):
        for load in mine_loads[step]:
            load.wait()
        for i in range(3):
            near_copy(step, i).wait_recv()
            for k in range(layers):
                for rows in blocks_of(parts[i]):
                    mix(step, k, rows, everything)
            if i == 1:
                for name in far_names[:early]:
                    far_start(step, name)
            elif i == 2:
                for name in far_names[early:]:
                    far_start(step, name)

    zeros = jnp.zeros((ROWS, width), jnp.float32)
    for side in (0, 1):
        @pl.when(jnp.logical_not(has_row[side]))
        def _():
            for i in range(3):
                fixed[i, halo_rows[side], :] = zeros
            for i in range(layers + 1):
                given[i, halo_rows[side], :] = zeros
            inner = slice(ROWS + halo_rows[side].start, ROWS + halo_rows[side].stop)
            for k in range(layers):
                field[0, k, inner, :] = zeros
                grad[STEPS - 1, k, inner, :] = zeros

    for past in (slice(0, ROWS), slice(extended + ROWS, extended + 2 * ROWS)):
        for step in range(STEPS):
            for k in range(layers):
                field[step, k, past, :] = zeros
                grad[step, k, past, :] = zeros
        for t in range(4):
            wr[t, past, :] = zeros

    last = chips - 1
    for load in mine_loads[last]:
        load.wait()
    for i in range(3):
        near_copy(last, i).wait_recv()

    small[1].wait()
    small[2].wait()
    speeds = []
    for k in range(layers):
        total = 0.0
        for c in range(speed_ref.shape[0]):
            total = jnp.where(class_ref[k] == c, speed_ref[c], total)
        speeds.append(total)

    upper = (lane >= LANES // 2).astype(jnp.int32)
    fixed_column().wait_recv()
    given_column().wait_recv()
    pl.when(has_outer(n))(outer_column().wait_recv)
    for a, (ref, i) in enumerate(shared):
        inner_ref = (fixed_inner, given_inner)[a >= 3]
        for r in range(0, height, ROWS):
            rows = slice(r, r + ROWS)
            back_by = lax.rem(2 * LANES - SHARE * (a + 1 - core), LANES)
            outer = jnp.where(has_outer(n), pltpu.roll(outer_recv[rows, :], back_by, 1), 0.0)
            ref[i, ROWS + r : 2 * ROWS + r, side_block] = jnp.where(
                upper == core, inner_ref[i, rows, :], outer
            )
    start(has_row, fixed_corner, final_row, given_row)

    def make_weights(b):
        rows = slice(b * ROWS, (b + 1) * ROWS)
        inner = slice((b + 1) * ROWS, (b + 2) * ROWS)
        row_w = stencil_weights(fixed[0, rows, :])
        col_w = stencil_weights(fixed[1, rows, :])
        for t, offset in enumerate(OFFSETS):
            wr[t, inner, :] = row_w[offset + 2]
            wc[t, rows, :] = col_w[offset + 2]
            wc_back[3 - t, rows, :] = pltpu.roll(col_w[offset + 2], offset % width, 1)
        centre[rows, :] = 1.0 + row_w[2] + col_w[2]

    def turn_weights(b):
        for t, offset in enumerate(OFFSETS):
            base = (b + 1) * ROWS + offset
            wr_back[t, b * ROWS : (b + 1) * ROWS, :] = wr[3 - t, base : base + ROWS, :]

    for b in all_blocks[1:-1]:
        make_weights(b)

    for b in inside:
        turn_weights(b)

    def chosen(k, rows, lanes):
        value = jnp.where(
            owner_ref[k] == n, mine[last, k, rows, lanes], near[last, k, rows, lanes]
        )
        for step in range(chips - 1):
            sender = lax.rem(chip + chips - 1 - step, chips)
            value = jnp.where(
                lax.div(owner_ref[k], pair) == sender, far[step, k, rows, lanes], value
            )
        return value

    def put(rows, lanes):
        for k in range(layers):
            for piece in halves_of(rows):
                field[0, k, shifted(piece), lanes] = chosen(k, piece, lanes)

    def halves_of(rows):
        return [slice(r, r + HALF) for r in range(rows.start, rows.stop, HALF)]

    def shifted(rows):
        return slice(2 * ROWS + rows.start, 2 * ROWS + rows.stop)

    swaps = [*rim, *inward, core_rows]

    def field_column(rows):
        at = swaps.index(rows)
        return remote(
            field.at[0, :, shifted(rows), inner_edge],
            field_inner.at[:, rows, :],
            col_sems.at[0, at],
            col_sems.at[1, at],
            partner,
        )

    halo_near = (
        slice(2 * ROWS - HALF, 2 * ROWS),
        slice(2 * ROWS + height, 2 * ROWS + height + HALF),
    )
    halo_beyond = (
        slice(ROWS, 2 * ROWS - HALF),
        slice(2 * ROWS + height + HALF, 3 * ROWS + height),
    )

    def field_row(side):
        return remote(
            field.at[0, :, shifted(rim[side]), 0:breadth],
            field.at[0, :, halo_near[1 - side], 0:breadth],
            row_sems.at[0, side],
            row_sems.at[1, 1 - side],
            row_device[side],
        )

    def field_corner(side):
        return remote(
            field.at[0, :, shifted(rim[side]), side_block],
            field.at[0, :, halo_near[1 - side], side_block],
            corner_sems.at[0, side],
            corner_sems.at[1, 1 - side],
            row_device[side],
        )

    def late_row(side):
        return remote(
            field.at[0, :, shifted(second[side]), :],
            field_late.at[1 - side],
            late_sems.at[0, side],
            late_sems.at[1, 1 - side],
            row_device[side],
        )

    def start_row(side, maker):
        pl.when(has_row[side])(maker(side).start)

    def take(name):
        for step in range(chips - 1):
            if name[0] == "outer":
                pl.when(has_outer(n))(far_copy(step, name).wait_recv)
            else:
                far_copy(step, name).wait_recv()

    def put_outer(rows):
        for k in range(layers):
            for piece in halves_of(rows):
                value = chosen(k, piece, side_block)
                field_outer[k, piece, :] = jnp.where(has_outer(n), value, 0.0)

    def join_field(rows):
        field_column(rows).wait_recv()
        for k in range(layers):
            for piece in halves_of(rows):
                field[0, k, shifted(piece), side_block] = jnp.where(
                    upper[:HALF] == core, field_inner[k, piece, :], field_outer[k, piece, :]
                )

    def take_rims(rows):
        for side in (0, 1):
            take(("edge", rows, side))
            put(rows, edge[side])
        field_column(rows).start()
        take(("outer", rows, 0))
        put_outer(rows)

    def take_main(rows):
        take(main_of(rows))
        put(rows, slice(LANES, breadth - LANES))

    for i in (0, 1):
        take_rims(rim[i])
    for i in (0, 1):
        take_main(rim[i])
        start_row(i, field_row)
        join_field(rim[i])
        start_row(i, field_corner)
    arrived(has_row, fixed_row, fixed_corner)
    make_weights(0)
    make_weights(all_blocks[-1])
    for i in (0, 1):
        take_rims(inward[i])
    for i in (0, 1):
        take_main(second[i])
        join_field(inward[i])
        start_row(i, late_row)
    take_rims(core_rows)
    for i in (0, 1):
        take_main(third[i])

    arrived(has_row, field_row, field_corner)

    def stencil(source, b, rows_w, cols_w):
        base = (b + 1) * ROWS
        rows = slice(b * ROWS, (b + 1) * ROWS)
        here = source[base : base + ROWS, :]
        total = centre[rows, :] * here
        for t, o in enumerate(OFFSETS):
            total += rows_w[t] * source[base + o : base + o + ROWS, :]
            total += cols_w[t] * pltpu.roll(here, (-o) % width, 1)
        return total

    def forward(step, b):
        rows = slice(b * ROWS, (b + 1) * ROWS)
        inner = slice((b + 1) * ROWS, (b + 2) * ROWS)
        rows_w = [wr[t, inner, :] for t in range(4)]
        cols_w = [wc[t, rows, :] for t in range(4)]
        above = None
        for k in range(layers):
            adv = stencil(field.at[step, k], b, rows_w, cols_w)
            square = adv * adv
            part = 1.0 / (1.0 + square)
            slope[step, k, rows, :] = speeds[k] * (1.0 - square) * part * part
            if step + 1 < STEPS:
                flux = speeds[k] * adv * part
                left = adv - flux
                if above is not None:
                    left = left + above
                field[step + 1, k, inner, :] = left * fixed[2, rows, :]
                above = flux

    def settle_back(step, b, adjoint, keep):
        rows = slice(b * ROWS, (b + 1) * ROWS)
        mask = fixed[2, rows, :]
        below = mask * given[layers, rows, :]
        for k in reversed(range(layers)):
            masked = adjoint[k] * mask
            keep(k, masked + (below - masked) * slope[step, k, rows, :])
            below = masked

    def keep_grad(step, b, first=0, last=ROWS):
        base = (b + 1) * ROWS

        def keep(k, value):
            grad[step, k, base + first : base + last, :] = value[first:last, :]

        return keep

    def back(step, b):
        rows = slice(b * ROWS, (b + 1) * ROWS)
        rows_w = [wr_back[t, rows, :] for t in range(4)]
        cols_w = [wc_back[t, rows, :] for t in range(4)]
        adjoint = [stencil(grad.at[step, k], b, rows_w, cols_w) for k in range(layers)]
        if step:
            settle_back(step - 1, b, adjoint, keep_grad(step - 1, b))
        else:
            spot = slice((b - 1) * ROWS, b * ROWS)
            for k in range(layers):
                out_ref[k, spot, :] = adjoint[k][:, 0:breadth]

    final_step = STEPS - 1

    def last_forward(b, keep):
        forward(final_step, b)
        rows = slice(b * ROWS, (b + 1) * ROWS)
        settle_back(final_step, b, [given[k, rows, :] for k in range(layers)], keep)

    def round_copy(side):
        return remote(
            round_send.at[side],
            round_recv.at[1 - side],
            round_sems.at[0, side],
            round_sems.at[1, 1 - side],
            row_device[side],
        )

    def receive_round(side):
        first = 2 * ROWS - 2 - HALF if side == 0 else 2 * ROWS + height + 2

        @pl.when(has_row[side])
        def _():
            round_copy(1 - side).wait_recv()
            for k in range(layers):
                grad[final_step, k, first : first + HALF, :] = round_recv[side, k]

    outside = (all_blocks[:2], all_blocks[-2:])
    for side in (0, 1):
        b = outside[side][1 - side]
        for at in (b - 1, b, b + 1):
            forward(0, at)
        for step in range(1, final_step):
            forward(step, b)
        first = 2 if side == 0 else ROWS - 2 - HALF

        def keep(k, value):
            round_send[side, k] = value[first : first + HALF, :]

        last_forward(b, keep)
        start_row(side, round_copy)

    take_main(core_rows)
    join_field(core_rows)
    for step in range(final_step):
        for b in inside:
            forward(step, b)
    for b in inside:
        last_forward(b, keep_grad(final_step, b))
    for side in (0, 1):
        @pl.when(has_row[side])
        def _():
            late_row(1 - side).wait_recv()
            for k in range(layers):
                field[0, k, halo_beyond[side], :] = field_late[side, k]

    ends = (all_blocks[0], all_blocks[-1])
    for step in range(final_step):
        for b in ends:
            forward(step, b)
    arrived(has_row, final_row, given_row)
    for side in (0, 1):
        b = outside[side][1 - side]
        last_forward(b, keep_grad(final_step, b))
        spot = (ROWS - 2, ROWS) if side == 0 else (0, 2)
        last_forward(ends[side], keep_grad(final_step, ends[side], *spot))
    for b in (*outside[0], *outside[1]):
        turn_weights(b)

    for step in range(final_step, 0, -1):
        for b in all_blocks[1:-1]:
            back(step, b)
    for b in inside:
        back(0, b)

    for side in (0, 1):
        receive_round(side)
        for step in range(final_step, 0, -1):
            for b in outside[side]:
                back(step, b)
    back(0, 1)
    back(0, own_blocks)

    def left(has, *makers):
        for side in (0, 1):
            @pl.when(has[side])
            def _():
                for maker in makers:
                    maker(side).wait_send()

    for step in range(chips):
        remote(give.at[step], near.at[step], near_sems.at[step, 3], near_sems.at[step, 0], partner).wait_send()
    for step in range(chips - 1):
        device = order[step] * pair + core
        for i, lanes in enumerate((slice(0, breadth), side_block)):
            sent = remote(
                mixed.at[step, :, :, lanes],
                far.at[step, :, :, lanes],
                far_sems.at[step, len(far_names) + i],
                far_sems.at[step, 0],
                (w, device),
            )
            if i == 0:
                sent.wait_send()
            else:
                pl.when(has_outer(device))(sent.wait_send)
    for rows in swaps:
        field_column(rows).wait_send()
    fixed_column().wait_send()
    given_column().wait_send()
    pl.when(has_outer(n))(outer_column().wait_send)
    left(
        has_row,
        fixed_row,
        fixed_corner,
        given_row,
        final_row,
        field_row,
        field_corner,
        late_row,
        round_copy,
    )


def body(group_wide, group, slots, owner, row_v, col_v, land_sea, layer_class, speed, final, deposit):
    layers, height, breadth = final.shape
    chips = group // 2
    hops = max(chips - 1, 1)
    f32 = jnp.float32
    extended = height + 2 * ROWS
    padded = extended + 2 * ROWS
    width = breadth + LANES
    dma = pltpu.SemaphoreType.DMA
    vmem = pl.BlockSpec(memory_space=pltpu.VMEM)
    hbm = pl.BlockSpec(memory_space=pltpu.HBM)
    return pl.pallas_call(
        functools.partial(kernel, group_wide, group),
        out_shape=pltpu.VMEM(final.shape, f32),
        in_specs=[hbm] * 9,
        out_specs=vmem,
        scratch_shapes=[
            pltpu.SMEM(owner.shape, owner.dtype),
            pltpu.SMEM(layer_class.shape, layer_class.dtype),
            pltpu.SMEM(speed.shape, speed.dtype),
            pltpu.VMEM(land_sea.shape, land_sea.dtype),
            pltpu.VMEM((3, extended, width), f32),
            pltpu.VMEM((3, height, LANES), f32),
            pltpu.VMEM((layers + 1, extended, width), f32),
            pltpu.VMEM((layers + 1, height, LANES), f32),
            pltpu.VMEM((height, LANES), f32),
            pltpu.VMEM((height, LANES), f32),
            pltpu.VMEM((chips, layers, height, width), f32),
            pltpu.VMEM((chips, layers, height, width), f32),
            pltpu.VMEM((chips, layers, height, width), f32),
            pltpu.VMEM((hops, layers, height, width), f32),
            pltpu.VMEM((hops, layers, height, width), f32),
            pltpu.VMEM((STEPS, layers, padded, width), f32),
            pltpu.VMEM((layers, height, LANES), f32),
            pltpu.VMEM((layers, height, LANES), f32),
            pltpu.VMEM((2, layers, HALF, width), f32),
            pltpu.VMEM((STEPS, layers, extended, width), f32),
            pltpu.VMEM((STEPS, layers, padded, width), f32),
            pltpu.VMEM((4, padded, width), f32),
            pltpu.VMEM((4, extended, width), f32),
            pltpu.VMEM((4, extended, width), f32),
            pltpu.VMEM((4, extended, width), f32),
            pltpu.VMEM((extended, width), f32),
            pltpu.VMEM((2, layers, HALF, width), f32),
            pltpu.VMEM((2, layers, HALF, width), f32),
            dma((8,)),
            dma((2, 2, chips)),
            dma((chips, 4)),
            dma((hops, 22 + 2)),
            dma((2, 3, 2)),
            dma((2, 3, 2)),
            dma((2, 5)),
            dma((2, 2)),
            dma((2, 2)),
            dma((2, 2)),
            dma((2, 2)),
        ],
        compiler_params=pltpu.CompilerParams(
            collective_id=0,
            has_side_effects=True,
            vmem_limit_bytes=VMEM_BYTES - final.size * final.dtype.itemsize,
        ),
    )(owner, layer_class, speed, slots, row_v, col_v, land_sea, final, deposit)


def solution(mesh):
    in_specs = (
        P("narrow", None, "wide", None),
        P(),
        P("wide", "narrow"),
        P("wide", "narrow"),
        P("wide", "narrow"),
        P(),
        P(),
        P(None, "wide", "narrow"),
        P("wide", "narrow"),
    )
    out_specs = P(None, "wide", "narrow")
    return jax.shard_map(
        functools.partial(body, mesh.shape["wide"], mesh.shape["narrow"]),
        mesh=mesh,
        in_specs=in_specs,
        out_specs=out_specs,
        check_vma=False,
    )
```

time: 21.6 us -> 18 us (0.83)
  the two profiles are of different devices: /device:TPU:10 before, /device:TPU:0 now
where the time goes in v2:
time: 18 us; the launch traced here: 17.8 us
  Pallas kernels  17.1 us (95%)
  local copies, waits for them, and re-layouts  0.71 us (4%)
    pallas_call x1, Pallas kernels, body(): pl.pallas_call(functools.partial(kernel, group_wide, group), out_shape=pl...  17.1 us
    unnamed x1, local copies, waits for them, and re-layouts  0.71 us

profile of v2, /device:TPU:0, one launch (start us, length us, event | category | flops | bytes accessed | tf_op | source)
XLA Modules:
  0.0 17.8 jit_solution(1957713619943507954)
XLA Ops:
  0.0 17.1 %shard_map.91 = f32[2,32,1024]{2,1,0:T(8,128)S(1)} custom-call(s32[2]{0:T(128)} %owner_hbm.1, s32[2]{0:T(128)} %class_hbm.1, f32[4]{0:T(128)} %speed_hbm.1, f32[1,2,32,4096]{3,2,1,0:T(8,128)} %slots_hbm.1, f32[32,1024]{1,0:T(8,128)} %row_velocity_hbm.1, f32[32,1024]{1,0:T(8,128)} %column_velocity_hbm.1, s32[32,1024]{1,0:T(8,128)} %sea_hbm.1, ...), custom_call_target="tpu_custom_call" | custom-call | tf_op jit(solution)/shard_map/pallas_call | solution.py:781
  17.1 0.7 %copy.11 = f32[2,32,1024]{2,1,0:T(8,128)} copy(f32[2,32,1024]{2,1,0:T(8,128)S(1)} %shard_map.91) | data formatting | bytes 524288

commit v3 on v2

--- a/solution.py
+++ b/solution.py
@@ -12,6 +12,7 @@
 ROWS = 8
 HALF = ROWS // 2
 SHARE = 16
+CHUNK = 3
 OFFSETS = (-2, -1, 1, 2)
 MESH = pl.DeviceIdType.MESH
 VMEM_BYTES = 67043328
@@ -70,6 +71,9 @@
     wr_back,
     wc_back,
     centre,
+    sea,
+    final_masked,
+    deposit_masked,
     round_send,
     round_recv,
     load_sems,
@@ -80,7 +84,6 @@
     given_sems,
     col_sems,
     row_sems,
-    corner_sems,
     late_sems,
     round_sems,
 ):
@@ -92,6 +95,7 @@
     chip = lax.div(n, pair)
     core = lax.rem(n, pair)
     width = breadth + LANES
+    tiles = breadth // LANES
     own_blocks = height // ROWS
     extended = height + 2 * ROWS
     all_blocks = list(range(own_blocks + 2))
@@ -140,7 +144,7 @@
         )
 
     small = [
-        pltpu.make_async_copy(source, target, load_sems.at[i])
+        pltpu.make_async_copy(source, target, load_sems.at[(0, 1, 2, 3, 3, 3, 4, 4)[i]])
         for i, (source, target) in enumerate(
             [
                 (owner_hbm, owner_ref),
@@ -160,17 +164,18 @@
                 pltpu.make_async_copy(
                     slots_hbm.at[0, :, :, columns(order[step] * pair + at_core)],
                     target.at[step, :, :, lanes],
-                    slot_sems.at[row, i, step],
+                    slot_sems.at[row, step],
                 )
-                for i, (columns, lanes) in enumerate(
-                    [
-                        (columns_of, slice(0, breadth)),
-                        (functools.partial(outer_columns, at_core=at_core), side_block),
-                    ]
-                )
+                for columns, lanes in [
+                    (columns_of, slice(0, breadth)),
+                    (functools.partial(outer_columns, at_core=at_core), side_block),
+                ]
             ]
             for step in range(chips)
         ]
+
+    def whole(ref, sem):
+        pltpu.make_async_copy(ref, ref, sem).wait()
 
     give_loads = slot_loads(give, 0, pair - 1 - core)
     mine_loads = slot_loads(mine, 1, core)
@@ -195,8 +200,8 @@
         return remote(
             give.at[step, :, parts[i], :],
             near.at[step, :, parts[i], :],
-            near_sems.at[step, 3],
-            near_sems.at[step, i],
+            near_sems.at[4 * step],
+            near_sems.at[4 * step + 1 + (i if step < chips - 1 else 0)],
             partner,
         )
 
@@ -209,11 +214,11 @@
         else:
             lanes = slice(LANES, breadth - LANES)
         spot = (slice(None), rows, lanes)
-        at = far_names.index(name)
+        at = far_groups.index((kind, rows))
         return remote(
             mixed.at[(step, *spot)],
             far.at[(step, *spot)],
-            far_sems.at[step, len(far_names) + int(kind == "outer")],
+            far_sems.at[step, len(far_groups) + int(kind == "outer")],
             far_sems.at[step, at],
             (w, order[step] * pair + core),
         )
@@ -236,6 +241,11 @@
     far_names += [main_of(third[i]) for i in (0, 1)]
     far_names += [main_of(core_rows)]
 
+    far_groups = []
+    for kind, rows, _ in far_names:
+        if (kind, rows) not in far_groups:
+            far_groups.append((kind, rows))
+
     def far_start(step, name):
         if name[0] == "outer":
             pl.when(has_outer(order[step] * pair + core))(far_copy(step, name).start)
@@ -243,8 +253,7 @@
             far_copy(step, name).start()
 
     for step in range(chips):
-        for load in give_loads[step]:
-            load.wait()
+        whole(give.at[step], slot_sems.at[0, step])
         for i in range(3):
             near_copy(step, i).start()
 
@@ -262,8 +271,8 @@
         return remote(
             fixed.at[:, source, 0:breadth],
             fixed.at[:, target, 0:breadth],
-            fixed_sems.at[0, 0, side],
-            fixed_sems.at[1, 0, 1 - side],
+            fixed_sems.at[0, side],
+            fixed_sems.at[1, 1 - side],
             row_device[side],
         )
 
@@ -271,8 +280,8 @@
         return remote(
             fixed.at[:, own, inner_edge],
             fixed_inner,
-            fixed_sems.at[0, 1, 0],
-            fixed_sems.at[1, 1, 0],
+            fixed_sems.at[0, 2],
+            fixed_sems.at[1, 2],
             partner,
         )
 
@@ -280,8 +289,8 @@
         return remote(
             given.at[:, own, inner_edge],
             given_inner,
-            given_sems.at[0, 0, 0],
-            given_sems.at[1, 0, 0],
+            given_sems.at[0, 2],
+            given_sems.at[1, 2],
             partner,
         )
 
@@ -289,8 +298,8 @@
         return remote(
             outer_send,
             outer_recv,
-            fixed_sems.at[0, 1, 1],
-            fixed_sems.at[1, 1, 1],
+            fixed_sems.at[0, 3],
+            fixed_sems.at[1, 3],
             (w, n - 1 + 2 * core),
         )
 
@@ -299,8 +308,8 @@
         return remote(
             fixed.at[:, source, side_block],
             fixed.at[:, target, side_block],
-            fixed_sems.at[0, 2, side],
-            fixed_sems.at[1, 2, 1 - side],
+            fixed_sems.at[0, side],
+            fixed_sems.at[1, 1 - side],
             row_device[side],
         )
 
@@ -309,8 +318,8 @@
         return remote(
             given.at[layers, source, :],
             given.at[layers, target, :],
-            given_sems.at[0, 1, side],
-            given_sems.at[1, 1, 1 - side],
+            given_sems.at[0, side],
+            given_sems.at[1, 1 - side],
             row_device[side],
         )
 
@@ -319,8 +328,28 @@
         return remote(
             given.at[0:layers, source, :],
             given.at[0:layers, target, :],
-            given_sems.at[0, 2, side],
-            given_sems.at[1, 2, 1 - side],
+            given_sems.at[0, side],
+            given_sems.at[1, 1 - side],
+            row_device[side],
+        )
+
+    def fixed_both(side):
+        source, target = near_edge(side, 0, ROWS - 2)
+        return remote(
+            fixed.at[:, source, :],
+            fixed.at[:, target, :],
+            fixed_sems.at[0, side],
+            fixed_sems.at[1, 1 - side],
+            row_device[side],
+        )
+
+    def given_both(side):
+        count = 2 * (STEPS - 1) + 2 * layers
+        return remote(
+            given.at[0, 0:count, :],
+            given.at[0, 0:count, :],
+            given_sems.at[0, side],
+            given_sems.at[1, 1 - side],
             row_device[side],
         )
 
@@ -338,16 +367,13 @@
                 for maker in makers:
                     maker(1 - side).wait_recv()
 
-    small[3].wait()
+    whole(fixed.at[:, own, 0:breadth], load_sems.at[3])
     for r in range(0, height, ROWS):
         fixed[2, ROWS + r : 2 * ROWS + r, 0:breadth] = sea_ref[r : r + ROWS, :].astype(jnp.float32)
-    small[4].wait()
-    small[5].wait()
 
     start(has_row, fixed_row)
     fixed_column().start()
-    small[6].wait()
-    small[7].wait()
+    whole(given.at[:, own, 0:breadth], load_sems.at[4])
     given_column().start()
     shared = [(fixed, i) for i in range(3)] + [(given, i) for i in range(layers + 1)]
     lane = lax.broadcasted_iota(jnp.int32, (ROWS, LANES), 1)
@@ -372,8 +398,7 @@
 
     everything = slice(0, width)
     for step in range(chips - 1):
-        for load in mine_loads[step]:
-            load.wait()
+        whole(mine.at[step], slot_sems.at[1, step])
         for i in range(3):
             near_copy(step, i).wait_recv()
             for k in range(layers):
@@ -387,6 +412,7 @@
                     far_start(step, name)
 
     zeros = jnp.zeros((ROWS, width), jnp.float32)
+    tile_zeros = jnp.zeros((tiles + 1, ROWS, LANES), jnp.float32)
     for side in (0, 1):
         @pl.when(jnp.logical_not(has_row[side]))
         def _():
@@ -396,22 +422,22 @@
                 given[i, halo_rows[side], :] = zeros
             inner = slice(ROWS + halo_rows[side].start, ROWS + halo_rows[side].stop)
             for k in range(layers):
-                field[0, k, inner, :] = zeros
-                grad[STEPS - 1, k, inner, :] = zeros
+                field[0, k, :, inner, :] = tile_zeros
+                grad[STEPS - 1, k, :, inner, :] = tile_zeros
 
     for past in (slice(0, ROWS), slice(extended + ROWS, extended + 2 * ROWS)):
         for step in range(STEPS):
             for k in range(layers):
-                field[step, k, past, :] = zeros
-                grad[step, k, past, :] = zeros
+                field[step, k, :, past, :] = tile_zeros
+                grad[step, k, :, past, :] = tile_zeros
         for t in range(4):
-            wr[t, past, :] = zeros
+            wr[t, :, past, :] = tile_zeros
 
     last = chips - 1
-    for load in mine_loads[last]:
-        load.wait()
-    for i in range(3):
-        near_copy(last, i).wait_recv()
+    whole(mine.at[last], slot_sems.at[1, last])
+    remote(
+        give.at[last], near.at[last], near_sems.at[4 * last], near_sems.at[4 * last + 1], partner
+    ).wait_recv()
 
     small[1].wait()
     small[2].wait()
@@ -437,27 +463,52 @@
             )
     start(has_row, fixed_corner, final_row, given_row)
 
+    def tiled(value):
+        return jnp.stack(
+            [value[:, j * LANES : (j + 1) * LANES] for j in range(value.shape[1] // LANES)]
+        )
+
+    wide_lane = lax.broadcasted_iota(jnp.int32, (tiles + 1, ROWS, LANES), 2)
+
+    def columns_off(value, offset):
+        turned = pltpu.roll(value, (-offset) % LANES, 2)
+        if offset > 0:
+            beside = jnp.concatenate([turned[1:], turned[:1]], axis=0)
+            return jnp.where(wide_lane < LANES - offset, turned, beside)
+        beside = jnp.concatenate([turned[-1:], turned[:-1]], axis=0)
+        return jnp.where(wide_lane >= -offset, turned, beside)
+
     def make_weights(b):
         rows = slice(b * ROWS, (b + 1) * ROWS)
         inner = slice((b + 1) * ROWS, (b + 2) * ROWS)
-        row_w = stencil_weights(fixed[0, rows, :])
-        col_w = stencil_weights(fixed[1, rows, :])
+        row_w = stencil_weights(tiled(fixed[0, rows, :]))
+        col_w = stencil_weights(tiled(fixed[1, rows, :]))
         for t, offset in enumerate(OFFSETS):
-            wr[t, inner, :] = row_w[offset + 2]
-            wc[t, rows, :] = col_w[offset + 2]
-            wc_back[3 - t, rows, :] = pltpu.roll(col_w[offset + 2], offset % width, 1)
-        centre[rows, :] = 1.0 + row_w[2] + col_w[2]
+            wr[t, :, inner, :] = row_w[offset + 2]
+            wc[t, :, rows, :] = col_w[offset + 2]
+            wc_back[3 - t, :, rows, :] = columns_off(col_w[offset + 2], -offset)
+        centre[:, rows, :] = 1.0 + row_w[2] + col_w[2]
+        sea[:, rows, :] = tiled(fixed[2, rows, :])
 
     def turn_weights(b):
         for t, offset in enumerate(OFFSETS):
             base = (b + 1) * ROWS + offset
-            wr_back[t, b * ROWS : (b + 1) * ROWS, :] = wr[3 - t, base : base + ROWS, :]
+            wr_back[t, :, b * ROWS : (b + 1) * ROWS, :] = wr[3 - t, :, base : base + ROWS, :]
 
     for b in all_blocks[1:-1]:
         make_weights(b)
 
+    def mask_given(b):
+        rows = slice(b * ROWS, (b + 1) * ROWS)
+        mask = sea[:, rows, :]
+        for k in range(layers):
+            final_masked[k, :, rows, :] = mask * tiled(given[k, rows, :])
+        deposit_masked[:, rows, :] = mask * tiled(given[layers, rows, :])
+
     for b in inside:
         turn_weights(b)
+    for b in all_blocks[1:-1]:
+        mask_given(b)
 
     def chosen(k, rows, lanes):
         value = jnp.where(
@@ -473,7 +524,11 @@
     def put(rows, lanes):
         for k in range(layers):
             for piece in halves_of(rows):
-                field[0, k, shifted(piece), lanes] = chosen(k, piece, lanes)
+                value = chosen(k, piece, lanes)
+                for j in range(value.shape[1] // LANES):
+                    field[0, k, lanes.start // LANES + j, shifted(piece), :] = value[
+                        :, j * LANES : (j + 1) * LANES
+                    ]
 
     def halves_of(rows):
         return [slice(r, r + HALF) for r in range(rows.start, rows.stop, HALF)]
@@ -486,10 +541,10 @@
     def field_column(rows):
         at = swaps.index(rows)
         return remote(
-            field.at[0, :, shifted(rows), inner_edge],
+            field.at[0, :, (1 - core) * (tiles - 1), shifted(rows), :],
             field_inner.at[:, rows, :],
-            col_sems.at[0, at],
-            col_sems.at[1, at],
+            col_sems.at[len(swaps)],
+            col_sems.at[at],
             partner,
         )
 
@@ -504,8 +559,8 @@
 
     def field_row(side):
         return remote(
-            field.at[0, :, shifted(rim[side]), 0:breadth],
-            field.at[0, :, halo_near[1 - side], 0:breadth],
+            field.at[0, :, 0:tiles, shifted(rim[side]), :],
+            field.at[0, :, 0:tiles, halo_near[1 - side], :],
             row_sems.at[0, side],
             row_sems.at[1, 1 - side],
             row_device[side],
@@ -513,19 +568,28 @@
 
     def field_corner(side):
         return remote(
-            field.at[0, :, shifted(rim[side]), side_block],
-            field.at[0, :, halo_near[1 - side], side_block],
-            corner_sems.at[0, side],
-            corner_sems.at[1, 1 - side],
+            field.at[0, :, tiles, shifted(rim[side]), :],
+            field.at[0, :, tiles, halo_near[1 - side], :],
+            row_sems.at[0, side],
+            row_sems.at[1, 1 - side],
+            row_device[side],
+        )
+
+    def field_both(side):
+        return remote(
+            field.at[0, :, :, shifted(rim[side]), :],
+            field.at[0, :, :, halo_near[1 - side], :],
+            row_sems.at[0, side],
+            row_sems.at[1, 1 - side],
             row_device[side],
         )
 
     def late_row(side):
         return remote(
-            field.at[0, :, shifted(second[side]), :],
+            field.at[0, :, :, shifted(second[side]), :],
             field_late.at[1 - side],
-            late_sems.at[0, side],
-            late_sems.at[1, 1 - side],
+            round_sems.at[0, side],
+            late_sems.at[1 - side],
             row_device[side],
         )
 
@@ -539,6 +603,17 @@
             else:
                 far_copy(step, name).wait_recv()
 
+    def take_edges(rows):
+        for step in range(chips - 1):
+            spot = (step, slice(None), rows, slice(0, 2 * LANES))
+            remote(
+                mixed.at[spot],
+                far.at[spot],
+                far_sems.at[step, len(far_groups)],
+                far_sems.at[step, far_groups.index(("edge", rows))],
+                (w, order[step] * pair + core),
+            ).wait_recv()
+
     def put_outer(rows):
         for k in range(layers):
             for piece in halves_of(rows):
@@ -549,13 +624,13 @@
         field_column(rows).wait_recv()
         for k in range(layers):
             for piece in halves_of(rows):
-                field[0, k, shifted(piece), side_block] = jnp.where(
+                field[0, k, tiles, shifted(piece), :] = jnp.where(
                     upper[:HALF] == core, field_inner[k, piece, :], field_outer[k, piece, :]
                 )
 
     def take_rims(rows):
+        take_edges(rows)
         for side in (0, 1):
-            take(("edge", rows, side))
             put(rows, edge[side])
         field_column(rows).start()
         take(("outer", rows, 0))
@@ -572,85 +647,123 @@
         start_row(i, field_row)
         join_field(rim[i])
         start_row(i, field_corner)
-    arrived(has_row, fixed_row, fixed_corner)
-    make_weights(0)
-    make_weights(all_blocks[-1])
     for i in (0, 1):
         take_rims(inward[i])
     for i in (0, 1):
         take_main(second[i])
         join_field(inward[i])
         start_row(i, late_row)
+    arrived(has_row, fixed_both)
+    make_weights(0)
+    make_weights(all_blocks[-1])
     take_rims(core_rows)
-    for i in (0, 1):
-        take_main(third[i])
-
-    arrived(has_row, field_row, field_corner)
-
-    def stencil(source, b, rows_w, cols_w):
-        base = (b + 1) * ROWS
-        rows = slice(b * ROWS, (b + 1) * ROWS)
-        here = source[base : base + ROWS, :]
-        total = centre[rows, :] * here
-        for t, o in enumerate(OFFSETS):
-            total += rows_w[t] * source[base + o : base + o + ROWS, :]
-            total += cols_w[t] * pltpu.roll(here, (-o) % width, 1)
-        return total
-
-    def forward(step, b):
-        rows = slice(b * ROWS, (b + 1) * ROWS)
-        inner = slice((b + 1) * ROWS, (b + 2) * ROWS)
-        rows_w = [wr[t, inner, :] for t in range(4)]
-        cols_w = [wc[t, rows, :] for t in range(4)]
-        above = None
-        for k in range(layers):
-            adv = stencil(field.at[step, k], b, rows_w, cols_w)
-            square = adv * adv
-            part = 1.0 / (1.0 + square)
-            slope[step, k, rows, :] = speeds[k] * (1.0 - square) * part * part
-            if step + 1 < STEPS:
-                flux = speeds[k] * adv * part
-                left = adv - flux
-                if above is not None:
-                    left = left + above
-                field[step + 1, k, inner, :] = left * fixed[2, rows, :]
-                above = flux
-
-    def settle_back(step, b, adjoint, keep):
-        rows = slice(b * ROWS, (b + 1) * ROWS)
-        mask = fixed[2, rows, :]
-        below = mask * given[layers, rows, :]
+    chunks = [slice(j, min(j + CHUNK, tiles + 1)) for j in range(0, tiles + 1, CHUNK)]
+
+    class Block:
+        def __init__(self, b):
+            self.first = b * ROWS
+
+        def load(self, ref, c, above=0, off=0):
+            first = self.first + above + off
+            return ref[c, first : first + ROWS, :]
+
+        def store(self, ref, c, value, above=0):
+            first = self.first + above
+            ref[c, first : first + ROWS, :] = value
+
+        def out(self, k, j, value):
+            first = self.first - ROWS
+            out_ref[k, first : first + ROWS, j * LANES : (j + 1) * LANES] = value
+
+    class Pair:
+        def __init__(self, depth):
+            self.top = ROWS + depth
+            self.bottom = ROWS + height - depth - HALF
+
+        def load(self, ref, c, above=0, off=0):
+            top = self.top + above + off
+            bottom = self.bottom + above + off - HALF
+            upper_rows = ref[c, top : top + ROWS, :]
+            sub = lax.broadcasted_iota(jnp.int32, upper_rows.shape, 1)
+            return jnp.where(sub < HALF, upper_rows, ref[c, bottom : bottom + ROWS, :])
+
+        def store(self, ref, c, value, above=0):
+            top, bottom = self.top + above, self.bottom + above
+            ref[c, top : top + HALF, :] = value[:, :HALF, :]
+            ref[c, bottom : bottom + HALF, :] = value[:, HALF:, :]
+
+        def out(self, k, j, value):
+            top, bottom = self.top - ROWS, self.bottom - ROWS
+            lanes = slice(j * LANES, (j + 1) * LANES)
+            out_ref[k, top : top + HALF, lanes] = value[:HALF, :]
+            out_ref[k, bottom : bottom + HALF, lanes] = value[HALF:, :]
+
+    chunks = [slice(j, min(j + CHUNK, tiles + 1)) for j in range(0, tiles + 1, CHUNK)]
+    full = slice(0, tiles + 1)
+
+    def stencils(sources, spot, rows_ref, rows_above, cols_ref):
+        here = [spot.load(source, full, ROWS) for source in sources]
+        moved = [[columns_off(value, o) for o in OFFSETS] for value in here]
+        for c in chunks:
+            rows_w = [spot.load(rows_ref.at[t], c, rows_above) for t in range(4)]
+            cols_w = [spot.load(cols_ref.at[t], c) for t in range(4)]
+            middle = spot.load(centre, c)
+            totals = []
+            for k, source in enumerate(sources):
+                total = middle * here[k][c]
+                for t, o in enumerate(OFFSETS):
+                    total += rows_w[t] * spot.load(source, c, ROWS, o)
+                    total += cols_w[t] * moved[k][t][c]
+                totals.append(total)
+            yield c, totals
+
+    def forward(step, spot):
+        sources = [field.at[step, k] for k in range(layers)]
+        for c, totals in stencils(sources, spot, wr, ROWS, wc):
+            above = None
+            for k, adv in enumerate(totals):
+                part = 1.0 / (1.0 + adv * adv)
+                settled = speeds[k] * part
+                spot.store(slope.at[step, k], c, settled * (2.0 * part - 1.0))
+                if step + 1 < STEPS:
+                    flux = settled * adv
+                    left = adv - flux
+                    if above is not None:
+                        left = left + above
+                    spot.store(field.at[step + 1, k], c, left * spot.load(sea, c), ROWS)
+                    above = flux
+
+    def settle_back(step, spot, c, masked, keep):
+        below = spot.load(deposit_masked, c)
         for k in reversed(range(layers)):
-            masked = adjoint[k] * mask
-            keep(k, masked + (below - masked) * slope[step, k, rows, :])
-            below = masked
-
-    def keep_grad(step, b, first=0, last=ROWS):
-        base = (b + 1) * ROWS
-
-        def keep(k, value):
-            grad[step, k, base + first : base + last, :] = value[first:last, :]
+            keep(k, c, masked[k] + (below - masked[k]) * spot.load(slope.at[step, k], c))
+            below = masked[k]
+
+    def keep_grad(step, spot):
+        def keep(k, c, value):
+            spot.store(grad.at[step, k], c, value, ROWS)
 
         return keep
 
-    def back(step, b):
-        rows = slice(b * ROWS, (b + 1) * ROWS)
-        rows_w = [wr_back[t, rows, :] for t in range(4)]
-        cols_w = [wc_back[t, rows, :] for t in range(4)]
-        adjoint = [stencil(grad.at[step, k], b, rows_w, cols_w) for k in range(layers)]
-        if step:
-            settle_back(step - 1, b, adjoint, keep_grad(step - 1, b))
-        else:
-            spot = slice((b - 1) * ROWS, b * ROWS)
-            for k in range(layers):
-                out_ref[k, spot, :] = adjoint[k][:, 0:breadth]
+    def back(step, spot):
+        sources = [grad.at[step, k] for k in range(layers)]
+        for c, adjoint in stencils(sources, spot, wr_back, 0, wc_back):
+            if step:
+                mask = spot.load(sea, c)
+                masked = [value * mask for value in adjoint]
+                settle_back(step - 1, spot, c, masked, keep_grad(step - 1, spot))
+            else:
+                for k in range(layers):
+                    for j in range(c.start, min(c.stop, tiles)):
+                        spot.out(k, j, adjoint[k][j - c.start])
 
     final_step = STEPS - 1
 
-    def last_forward(b, keep):
-        forward(final_step, b)
-        rows = slice(b * ROWS, (b + 1) * ROWS)
-        settle_back(final_step, b, [given[k, rows, :] for k in range(layers)], keep)
+    def last_forward(spot, keep):
+        forward(final_step, spot)
+        for c in chunks:
+            masked = [spot.load(final_masked.at[k], c) for k in range(layers)]
+            settle_back(final_step, spot, c, masked, keep)
 
     def round_copy(side):
         return remote(
@@ -661,6 +774,15 @@
             row_device[side],
         )
 
+    def round_both(side):
+        return remote(
+            round_send,
+            round_recv,
+            round_sems.at[0, side],
+            round_sems.at[1, 1 - side],
+            row_device[side],
+        )
+
     def receive_round(side):
         first = 2 * ROWS - 2 - HALF if side == 0 else 2 * ROWS + height + 2
 
@@ -668,64 +790,33 @@
         def _():
             round_copy(1 - side).wait_recv()
             for k in range(layers):
-                grad[final_step, k, first : first + HALF, :] = round_recv[side, k]
-
-    outside = (all_blocks[:2], all_blocks[-2:])
+                grad[final_step, k, :, first : first + HALF, :] = round_recv[side, k]
+
+    arrived(has_row, field_both)
+    for b in (all_blocks[0], all_blocks[-1]):
+        forward(0, Block(b))
     for side in (0, 1):
-        b = outside[side][1 - side]
-        for at in (b - 1, b, b + 1):
-            forward(0, at)
+        b = all_blocks[-2] if side else all_blocks[1]
+        take_main(third[side])
+        forward(0, Block(b))
+        forward(0, Block(b + 1 - 2 * side))
         for step in range(1, final_step):
-            forward(step, b)
+            forward(step, Block(b))
         first = 2 if side == 0 else ROWS - 2 - HALF
 
-        def keep(k, value):
-            round_send[side, k] = value[first : first + HALF, :]
-
-        last_forward(b, keep)
+        def keep_round(k, c, value):
+            round_send[side, k, c] = value[:, first : first + HALF, :]
+
+        last_forward(Block(b), keep_round)
         start_row(side, round_copy)
 
     take_main(core_rows)
     join_field(core_rows)
     for step in range(final_step):
         for b in inside:
-            forward(step, b)
+            forward(step, Block(b))
     for b in inside:
-        last_forward(b, keep_grad(final_step, b))
-    for side in (0, 1):
-        @pl.when(has_row[side])
-        def _():
-            late_row(1 - side).wait_recv()
-            for k in range(layers):
-                field[0, k, halo_beyond[side], :] = field_late[side, k]
-
-    ends = (all_blocks[0], all_blocks[-1])
-    for step in range(final_step):
-        for b in ends:
-            forward(step, b)
-    arrived(has_row, final_row, given_row)
-    for side in (0, 1):
-        b = outside[side][1 - side]
-        last_forward(b, keep_grad(final_step, b))
-        spot = (ROWS - 2, ROWS) if side == 0 else (0, 2)
-        last_forward(ends[side], keep_grad(final_step, ends[side], *spot))
-    for b in (*outside[0], *outside[1]):
-        turn_weights(b)
-
-    for step in range(final_step, 0, -1):
-        for b in all_blocks[1:-1]:
-            back(step, b)
-    for b in inside:
-        back(0, b)
-
-    for side in (0, 1):
-        receive_round(side)
-        for step in range(final_step, 0, -1):
-            for b in outside[side]:
-                back(step, b)
-    back(0, 1)
-    back(0, own_blocks)
-
+        last_forward(Block(b), keep_grad(final_step, Block(b)))
     def left(has, *makers):
         for side in (0, 1):
             @pl.when(has[side])
@@ -734,14 +825,16 @@
                     maker(side).wait_send()
 
     for step in range(chips):
-        remote(give.at[step], near.at[step], near_sems.at[step, 3], near_sems.at[step, 0], partner).wait_send()
+        remote(
+            give.at[step], near.at[step], near_sems.at[4 * step], near_sems.at[4 * step + 1], partner
+        ).wait_send()
     for step in range(chips - 1):
         device = order[step] * pair + core
         for i, lanes in enumerate((slice(0, breadth), side_block)):
             sent = remote(
                 mixed.at[step, :, :, lanes],
                 far.at[step, :, :, lanes],
-                far_sems.at[step, len(far_names) + i],
+                far_sems.at[step, len(far_groups) + i],
                 far_sems.at[step, 0],
                 (w, device),
             )
@@ -749,22 +842,47 @@
                 sent.wait_send()
             else:
                 pl.when(has_outer(device))(sent.wait_send)
-    for rows in swaps:
-        field_column(rows).wait_send()
+    remote(
+        field.at[0, :, (1 - core) * (tiles - 1), shifted(slice(0, height)), :],
+        field_inner,
+        col_sems.at[len(swaps)],
+        col_sems.at[0],
+        partner,
+    ).wait_send()
     fixed_column().wait_send()
     given_column().wait_send()
     pl.when(has_outer(n))(outer_column().wait_send)
-    left(
-        has_row,
-        fixed_row,
-        fixed_corner,
-        given_row,
-        final_row,
-        field_row,
-        field_corner,
-        late_row,
-        round_copy,
-    )
+    left(has_row, fixed_both, given_both, field_both)
+
+    for side in (0, 1):
+        @pl.when(has_row[side])
+        def _():
+            late_row(1 - side).wait_recv()
+            for k in range(layers):
+                field[0, k, :, halo_beyond[side], :] = field_late[side, k]
+
+    ends = (all_blocks[0], all_blocks[-1])
+    for step in range(final_step):
+        for b in ends:
+            forward(step, Block(b))
+    arrived(has_row, given_both)
+    for b in ends:
+        mask_given(b)
+    for b in (all_blocks[1], all_blocks[-2]):
+        last_forward(Block(b), keep_grad(final_step, Block(b)))
+    last_forward(Pair(-HALF), keep_grad(final_step, Pair(-HALF)))
+    for b in (*all_blocks[:2], *all_blocks[-2:]):
+        turn_weights(b)
+
+    for step in range(final_step, -1, -1):
+        for b in all_blocks[1:-1]:
+            back(step, Block(b))
+    for side in (0, 1):
+        receive_round(side)
+    for step in range(final_step, -1, -1):
+        back(step, Pair(-2 * step))
+
+    left(has_row, round_both)
 
 
 def body(group_wide, group, slots, owner, row_v, col_v, land_sea, layer_class, speed, final, deposit):
@@ -775,6 +893,7 @@
     extended = height + 2 * ROWS
     padded = extended + 2 * ROWS
     width = breadth + LANES
+    tiles = width // LANES
     dma = pltpu.SemaphoreType.DMA
     vmem = pl.BlockSpec(memory_space=pltpu.VMEM)
     hbm = pl.BlockSpec(memory_space=pltpu.HBM)
@@ -799,29 +918,31 @@
             pltpu.VMEM((chips, layers, height, width), f32),
             pltpu.VMEM((hops, layers, height, width), f32),
             pltpu.VMEM((hops, layers, height, width), f32),
-            pltpu.VMEM((STEPS, layers, padded, width), f32),
+            pltpu.VMEM((STEPS, layers, tiles, padded, LANES), f32),
             pltpu.VMEM((layers, height, LANES), f32),
             pltpu.VMEM((layers, height, LANES), f32),
-            pltpu.VMEM((2, layers, HALF, width), f32),
-            pltpu.VMEM((STEPS, layers, extended, width), f32),
-            pltpu.VMEM((STEPS, layers, padded, width), f32),
-            pltpu.VMEM((4, padded, width), f32),
-            pltpu.VMEM((4, extended, width), f32),
-            pltpu.VMEM((4, extended, width), f32),
-            pltpu.VMEM((4, extended, width), f32),
-            pltpu.VMEM((extended, width), f32),
-            pltpu.VMEM((2, layers, HALF, width), f32),
-            pltpu.VMEM((2, layers, HALF, width), f32),
-            dma((8,)),
-            dma((2, 2, chips)),
-            dma((chips, 4)),
-            dma((hops, 22 + 2)),
-            dma((2, 3, 2)),
-            dma((2, 3, 2)),
-            dma((2, 5)),
+            pltpu.VMEM((2, layers, tiles, HALF, LANES), f32),
+            pltpu.VMEM((STEPS, layers, tiles, extended, LANES), f32),
+            pltpu.VMEM((STEPS, layers, tiles, padded, LANES), f32),
+            pltpu.VMEM((4, tiles, padded, LANES), f32),
+            pltpu.VMEM((4, tiles, extended, LANES), f32),
+            pltpu.VMEM((4, tiles, extended, LANES), f32),
+            pltpu.VMEM((4, tiles, extended, LANES), f32),
+            pltpu.VMEM((tiles, extended, LANES), f32),
+            pltpu.VMEM((tiles, extended, LANES), f32),
+            pltpu.VMEM((layers, tiles, extended, LANES), f32),
+            pltpu.VMEM((tiles, extended, LANES), f32),
+            pltpu.VMEM((2, layers, tiles, HALF, LANES), f32),
+            pltpu.VMEM((2, layers, tiles, HALF, LANES), f32),
+            dma((5,)),
+            dma((2, chips)),
+            dma((4 * (chips - 1) + 2,)),
+            dma((hops, 17 + 2)),
+            dma((2, 4)),
+            dma((2, 3)),
+            dma((6,)),
             dma((2, 2)),
-            dma((2, 2)),
-            dma((2, 2)),
+            dma((2,)),
             dma((2, 2)),
         ],
         compiler_params=pltpu.CompilerParams(

time: 18 us -> 17.6 us (0.978)
  Pallas kernels: 17.1 us -> 16.7 us
    pallas_call x1, Pallas kernels: 17.1 us -> 16.7 us  [body(): pl.pallas_call(functools.partial(kernel, group_wide, group), out_shape=pl...]
where the time goes in v3:
time: 17.6 us; the launch traced here: 17.4 us
  Pallas kernels  16.7 us (95%)
  local copies, waits for them, and re-layouts  0.71 us (4%)
    pallas_call x1, Pallas kernels, body(): pl.pallas_call(functools.partial(kernel, group_wide, group), out_shape=pl...  16.7 us
    unnamed x1, local copies, waits for them, and re-layouts  0.71 us

profile of v3, /device:TPU:0, one launch (start us, length us, event | category | flops | bytes accessed | tf_op | source)
XLA Modules:
  0.0 17.4 jit_solution(4604045835901359161)
XLA Ops:
  0.0 16.7 %shard_map.91 = f32[2,32,1024]{2,1,0:T(8,128)S(1)} custom-call(s32[2]{0:T(128)} %owner_hbm.1, s32[2]{0:T(128)} %class_hbm.1, f32[4]{0:T(128)} %speed_hbm.1, f32[1,2,32,4096]{3,2,1,0:T(8,128)} %slots_hbm.1, f32[32,1024]{1,0:T(8,128)} %row_velocity_hbm.1, f32[32,1024]{1,0:T(8,128)} %column_velocity_hbm.1, s32[32,1024]{1,0:T(8,128)} %sea_hbm.1, ...), custom_call_target="tpu_custom_call" | custom-call | tf_op jit(solution)/shard_map/pallas_call | solution.py:900
  16.7 0.7 %copy.11 = f32[2,32,1024]{2,1,0:T(8,128)} copy(f32[2,32,1024]{2,1,0:T(8,128)S(1)} %shard_map.91) | data formatting | bytes 524288

commit v4 on v3

--- a/solution.py
+++ b/solution.py
@@ -313,25 +313,28 @@
             row_device[side],
         )
 
-    def given_row(side):
-        source, target = near_edge(side, 0, 2 * (STEPS - 1))
-        return remote(
-            given.at[layers, source, :],
-            given.at[layers, target, :],
-            given_sems.at[0, side],
-            given_sems.at[1, 1 - side],
-            row_device[side],
-        )
-
-    def final_row(side):
-        source, target = near_edge(side, 0, 2)
-        return remote(
-            given.at[0:layers, source, :],
-            given.at[0:layers, target, :],
-            given_sems.at[0, side],
-            given_sems.at[1, 1 - side],
-            row_device[side],
-        )
+    def given_rows(lanes):
+        def deposit_rows(side):
+            source, target = near_edge(side, 0, 2 * (STEPS - 1))
+            return remote(
+                given.at[layers, source, lanes],
+                given.at[layers, target, lanes],
+                given_sems.at[0, side],
+                given_sems.at[1, 1 - side],
+                row_device[side],
+            )
+
+        def final_rows(side):
+            source, target = near_edge(side, 0, 2)
+            return remote(
+                given.at[0:layers, source, lanes],
+                given.at[0:layers, target, lanes],
+                given_sems.at[0, side],
+                given_sems.at[1, 1 - side],
+                row_device[side],
+            )
+
+        return final_rows, deposit_rows
 
     def fixed_both(side):
         source, target = near_edge(side, 0, ROWS - 2)
@@ -374,6 +377,7 @@
     start(has_row, fixed_row)
     fixed_column().start()
     whole(given.at[:, own, 0:breadth], load_sems.at[4])
+    start(has_row, *given_rows(slice(0, breadth)))
     given_column().start()
     shared = [(fixed, i) for i in range(3)] + [(given, i) for i in range(layers + 1)]
     lane = lax.broadcasted_iota(jnp.int32, (ROWS, LANES), 1)
@@ -461,7 +465,7 @@
             ref[i, ROWS + r : 2 * ROWS + r, side_block] = jnp.where(
                 upper == core, inner_ref[i, rows, :], outer
             )
-    start(has_row, fixed_corner, final_row, given_row)
+    start(has_row, fixed_corner, *given_rows(side_block))
 
     def tiled(value):
         return jnp.stack(
@@ -793,8 +797,7 @@
                 grad[final_step, k, :, first : first + HALF, :] = round_recv[side, k]
 
     arrived(has_row, field_both)
-    for b in (all_blocks[0], all_blocks[-1]):
-        forward(0, Block(b))
+    forward(0, Pair(-HALF))
     for side in (0, 1):
         b = all_blocks[-2] if side else all_blocks[1]
         take_main(third[side])

time: 17.6 us -> 17.5 us (level)
  no operation moved by 1% of the time
where the time goes in v4:
time: 17.5 us; the launch traced here: 17.4 us
  Pallas kernels  16.7 us (95%)
  local copies, waits for them, and re-layouts  0.71 us (4%)
    pallas_call x1, Pallas kernels, body(): pl.pallas_call(functools.partial(kernel, group_wide, group), out_shape=pl...  16.7 us
    unnamed x1, local copies, waits for them, and re-layouts  0.71 us

profile of v4, /device:TPU:0, one launch (start us, length us, event | category | flops | bytes accessed | tf_op | source)
XLA Modules:
  0.0 17.4 jit_solution(12859513472576303405)
XLA Ops:
  0.0 16.7 %shard_map.91 = f32[2,32,1024]{2,1,0:T(8,128)S(1)} custom-call(s32[2]{0:T(128)} %owner_hbm.1, s32[2]{0:T(128)} %class_hbm.1, f32[4]{0:T(128)} %speed_hbm.1, f32[1,2,32,4096]{3,2,1,0:T(8,128)} %slots_hbm.1, f32[32,1024]{1,0:T(8,128)} %row_velocity_hbm.1, f32[32,1024]{1,0:T(8,128)} %column_velocity_hbm.1, s32[32,1024]{1,0:T(8,128)} %sea_hbm.1, ...), custom_call_target="tpu_custom_call" | custom-call | tf_op jit(solution)/shard_map/pallas_call | solution.py:903
  16.7 0.7 %copy.11 = f32[2,32,1024]{2,1,0:T(8,128)} copy(f32[2,32,1024]{2,1,0:T(8,128)S(1)} %shard_map.91) | data formatting | bytes 524288
